TPU v7x, 128 devices: a whole 4x4x4 slice. The times are simulated.
128 devices in a mesh: dp: 4 (over z), expert: 16 (over y, x_hi, core), tensor: 2 (over x_lo).
Axes of the slice: x: 4 (x_hi: 2, x_lo: 2; x = x_hi * 2 + x_lo), y: 4, z: 4, core: 2. Of those that a mesh axis runs over, the one named last changes fastest.
Arguments:
- hidden: bfloat16 [8192, 6144], P(('dp', 'expert'), 'tensor'), may hold values from -6 to 6
- expert_ids: int32 [8192, 8], P(('dp', 'expert')), may hold values from 0 to 383, as said below
- gate_fixed: int32 [8192, 8], P(('dp', 'expert')), may hold values from 4096 to 65535
- slot_expert: int32 [64], replicated, may hold values from 0 to 383, as said below
- expert_in: bfloat16 [64, 6144, 2, 1024], P(('dp', 'expert'), 'tensor'), may hold values from -1 to 1, as said below
- expert_out: bfloat16 [64, 1024, 6144], P(('dp', 'expert'), None, 'tensor'), may hold values from -1 to 1, as said below
- shared_in: bfloat16 [6144, 2, 1024], P('tensor', None, 'dp'), may hold values from -0.078125 to 0.078125
- shared_out: bfloat16 [1024, 6144], P('dp', 'tensor'), may hold values from -0.1875 to 0.1875
Outputs:
- mixed: bfloat16 [8192, 6144], P(('dp', 'expert'), 'tensor')
Inputs may be any that keep to these rules, and one draw needn't show every extreme that they name: `expert_ids`: each row names 8 different experts. `slot_expert`: 56 different experts fill the 64 slots; 8 of them hold two slots each, the others one. `expert_in`: slots that hold the same expert hold the same weights. `expert_out`: slots that hold the same expert hold the same weights.
All inputs are finite; a program needn't handle non-finite values.
Results may differ from a plain program's by a relative error of at most 0.006.
Values may be sent and summed in bfloat16 or wider, within the bound.
No kernel may reach another device: no remote copies, remote signals or barrier semaphores. Data moves between devices by JAX's collectives and lax.ppermute only.
A program may use at most 192 MiB of HBM per device.

v0:
```python
import functools

import jax
import jax.numpy as jnp
from jax import lax
from jax.experimental import pallas as pl
from jax.experimental.pallas import tpu as pltpu
from jax.sharding import PartitionSpec as P


CAP = 4
BF = jnp.bfloat16
F32 = jnp.float32


def params(mib=20):
    return pltpu.CompilerParams(vmem_limit_bytes=mib * 2**20)


def far(array):
    return pltpu.with_memory_space_constraint(array, pltpu.HBM)


def dot(a, b):
    return jnp.dot(a, b, preferred_element_type=F32)


def iota(shape, dim):
    return lax.broadcasted_iota(jnp.int32, shape, dim)


def silu_mul(gate, up):
    return (jax.nn.silu(gate) * up).astype(BF)


def route_kernel(ids, gates, held_row, left, right, rows_out, high_out, low_out, pick):
    slots = held_row.shape[1]
    fold = 2 * CAP
    lanes = slots * fold
    tokens = ids.shape[1]

    @pl.when(pl.program_id(0) == 0)
    def _():
        row, col = iota((lanes, slots), 0), iota((lanes, slots), 1)
        held_all = jnp.broadcast_to(held_row[...], (lanes, slots))
        held = jnp.max(jnp.where(col == row // fold, held_all, -1), axis=1, keepdims=True)
        twin = (held_all == held) & (col < row // fold)
        spare = jnp.max(jnp.where(twin, CAP, 0), axis=1, keepdims=True)
        named = jnp.zeros((lanes, tokens), jnp.float32)
        gate = jnp.zeros((lanes, tokens), jnp.int32)
        for k in range(ids.shape[0]):
            hit = ids[k : k + 1, :] == held
            named = jnp.where(hit, 1.0, named)
            gate = gate + jnp.where(hit, gates[k : k + 1, :], 0)
        earlier = iota((tokens, tokens), 0) < iota((tokens, tokens), 1)
        rank = dot(named.astype(BF), jnp.where(earlier, 1.0, 0.0).astype(BF)).astype(jnp.int32)
        row = iota((lanes, tokens), 0)
        served = (named > 0.5) & (rank - spare == row % CAP)
        is_left = row % fold < CAP
        pick[0] = jnp.where(served & is_left, 1.0, 0.0).astype(BF)
        pick[1] = jnp.where(served & ~is_left, 1.0, 0.0).astype(BF)
        high = jnp.where(served, gate // 256, 0).astype(F32) * 2.0**-8
        low = jnp.where(served, gate % 256, 0).astype(F32) * 2.0**-16
        high_out[...] = high.astype(BF)
        low_out[...] = low.astype(BF)

    rows_out[...] = (dot(pick[0], left[...]) + dot(pick[1], right[...])).astype(BF)


def route(ids, gates, slot_expert, hidden, block=512):
    slots = slot_expert.shape[0]
    lanes = slots * 2 * CAP
    tokens, width = hidden.shape
    half = width // 2
    blocks = half // block

    def whole(*shape):
        return pl.BlockSpec(shape, lambda j: (0, 0))

    return pl.pallas_call(
        route_kernel,
        grid=(blocks,),
        in_specs=[
            whole(ids.shape[1], tokens),
            whole(ids.shape[1], tokens),
            whole(1, slots),
            pl.BlockSpec((tokens, block), lambda j: (0, j)),
            pl.BlockSpec((tokens, block), lambda j: (0, blocks + j)),
        ],
        out_specs=(
            pl.BlockSpec((lanes, block), lambda j: (0, j)),
            whole(lanes, tokens),
            whole(lanes, tokens),
        ),
        out_shape=(
            pltpu.HBM((lanes, half), BF),
            pltpu.HBM((lanes, tokens), BF),
            pltpu.HBM((lanes, tokens), BF),
        ),
        scratch_shapes=[pltpu.VMEM((2, lanes, tokens), BF)],
        compiler_params=params(16),
        name="route",
    )(*(far(x) for x in (ids.T, gates.T, slot_expert[None], hidden, hidden)))


def split_kernel(w, out, *, sub, paired):
    depth, _, units = w.shape
    blocks, _, block = out.shape
    row, col = iota((2 * sub, 2 * sub), 0), iota((2 * sub, 2 * sub), 1)
    source = jnp.where(row < sub, 2 * row, 2 * (row - sub) + 1)
    order = jnp.where(col == source, 1.0, 0.0).astype(BF)
    for start in range(0, depth, sub):
        rows = w[start : start + sub].reshape(2 * sub, units)
        moved = dot(order, rows).astype(BF)
        here = slice(start, start + sub)
        part = block // 2 if paired else block
        for j in range(units // part):
            cols = slice(j * part, (j + 1) * part)
            if paired:
                out[j, here, :part] = moved[:sub, cols]
                out[j, here, part:] = moved[sub:, cols]
            else:
                out[j, here, :] = moved[:sub, cols]
                out[blocks // 2 + j, here, :] = moved[sub:, cols]


def split_gate_up(w, block, paired, part=0, parts=1, depth=512, sub=128):
    _, _, units = w.shape
    width = w.shape[0] // parts
    first = part * (width // depth)
    blocks = 2 * units // block
    return pl.pallas_call(
        functools.partial(split_kernel, sub=sub, paired=paired),
        grid=(width // depth,),
        in_specs=[pl.BlockSpec((depth, 2, units), lambda i: (first + i, 0, 0))],
        out_specs=pl.BlockSpec((blocks, depth, block), lambda i: (0, i, 0)),
        out_shape=pltpu.HBM((blocks, width, block), BF),
        compiler_params=params(20),
        name="split",
    )(far(w))


def unfold_kernel(me, arrived, w_left, w_right, x_out, part_out):
    @pl.when(pl.program_id(0) == 0)
    def _():
        half = arrived.shape[1]
        rows = arrived.shape[0] // 2
        row, col = iota((rows, 2 * rows), 0), iota((rows, 2 * rows), 1)
        first = row // CAP * (2 * CAP) + row % CAP
        for h in range(2):
            pick = jnp.where(col == first + h * CAP, 1.0, 0.0).astype(BF)
            x_out[:, h * half : (h + 1) * half] = dot(pick, arrived[...]).astype(BF)

    part_out[...] = halves_dot(x_out, w_left, w_right).astype(part_out.dtype)


def halves_dot(x, w_left, w_right):
    half = w_left.shape[1]
    return dot(x[:, :half], w_left[0]) + dot(x[:, half:], w_right[0])


def half_block(j, mine, blocks):
    return j // blocks * 2 * blocks + mine * blocks + j % blocks


def send_half(arrived, w, me):
    lanes, half = arrived.shape
    rows, block = lanes // 2, w[0].shape[2]
    blocks = w[0].shape[0] // 4
    units = 2 * blocks * block
    return pl.pallas_call(
        unfold_kernel,
        grid_spec=pltpu.PrefetchScalarGridSpec(
            num_scalar_prefetch=1,
            grid=(2 * blocks,),
            in_specs=[
                pl.BlockSpec((lanes, half), lambda j, me: (0, 0)),
            ]
            + [
                pl.BlockSpec(
                    (1, half, block), lambda j, me: (half_block(j, 1 - me[0], blocks), 0, 0)
                )
            ]
            * 2,
            out_specs=(
                pl.BlockSpec((rows, 2 * half), lambda j, me: (0, 0)),
                pl.BlockSpec((rows, block), lambda j, me: (0, j)),
            ),
        ),
        out_shape=(
            jax.ShapeDtypeStruct((rows, 2 * half), BF),
            jax.ShapeDtypeStruct((rows, units), BF),
        ),
        compiler_params=params(),
        name="send_half",
    )(me, arrived, far(w[0]), far(w[1]))


def keep_kernel(me, x, w_left, w_right, out):
    out[...] = halves_dot(x, w_left, w_right)


def keep_half(x, w, me):
    rows, width = x.shape
    block = w[0].shape[2]
    blocks = w[0].shape[0] // 4
    units = 2 * blocks * block
    return pl.pallas_call(
        keep_kernel,
        grid_spec=pltpu.PrefetchScalarGridSpec(
            num_scalar_prefetch=1,
            grid=(2 * blocks,),
            in_specs=[
                pl.BlockSpec((rows, width), lambda j, me: (0, 0)),
            ]
            + [
                pl.BlockSpec(
                    (1, width // 2, block), lambda j, me: (half_block(j, me[0], blocks), 0, 0)
                )
            ]
            * 2,
            out_specs=pl.BlockSpec((rows, block), lambda j, me: (0, j)),
        ),
        out_shape=jax.ShapeDtypeStruct((rows, units), F32),
        compiler_params=params(),
        name="keep_half",
    )(me, x, far(w[0]), far(w[1]))


def act_kernel(kept, came, out):
    units = out.shape[1]
    pre = kept[...] + came[...].astype(F32)
    out[...] = silu_mul(pre[:, :units], pre[:, units:])


def activate(kept, came):
    rows, units = kept.shape
    return pl.pallas_call(
        act_kernel,
        out_shape=jax.ShapeDtypeStruct((rows, units // 2), BF),
        compiler_params=params(),
        name="activate",
    )(kept, came)


def answer_kernel(me, mine, other, w_mine_l, w_other_l, w_mine_r, w_other_r, out):
    rows = mine.shape[0]
    row, col = iota((2 * rows, rows), 0), iota((2 * rows, rows), 1)
    first = col // CAP * (2 * CAP) + col % CAP
    total = jnp.zeros(out.shape, F32)
    for h, (wm, wo) in enumerate(((w_mine_l, w_other_l), (w_mine_r, w_other_r))):
        answer = (dot(mine[...], wm[...]) + dot(other[...], wo[...])).astype(BF)
        total += dot(jnp.where(row == first + h * CAP, 1.0, 0.0).astype(BF), answer)
    out[...] = total.astype(BF)


def answers(mine, other, w, me, block=512):
    rows, units = mine.shape
    width = w.shape[1]
    blocks = width // 2 // block

    def part(side, h):
        return pl.BlockSpec(
            (units, block),
            lambda n, me: ((me[0] if side else 1 - me[0]), h * blocks + n),
        )

    whole = pl.BlockSpec((rows, units), lambda n, me: (0, 0))
    return pl.pallas_call(
        answer_kernel,
        grid_spec=pltpu.PrefetchScalarGridSpec(
            num_scalar_prefetch=1,
            grid=(blocks,),
            in_specs=[whole, whole, part(1, 0), part(0, 0), part(1, 1), part(0, 1)],
            out_specs=pl.BlockSpec((2 * rows, block), lambda n, me: (0, n)),
        ),
        out_shape=pltpu.HBM((2 * rows, width // 2), BF),
        compiler_params=params(),
        name="answers",
    )(me, mine, other, *(far(w),) * 4)


def shared_kernel(*refs):
    *pieces, w, sent, kept = refs
    start = 0
    for piece in pieces:
        rows = slice(start, start + piece.shape[0])
        start += piece.shape[0]
        pre = dot(piece[...], w[0])
        sent[rows, :] = pre.astype(BF)
        kept[rows, :] = pre


def shared_in_part(pieces, w):
    rows = sum(piece.shape[0] for piece in pieces)
    blocks, width, block = w.shape
    part = pl.BlockSpec((rows, block), lambda j: (0, j))
    return pl.pallas_call(
        shared_kernel,
        grid=(blocks,),
        in_specs=[pl.BlockSpec(memory_space=pltpu.VMEM)] * len(pieces)
        + [pl.BlockSpec((1, width, block), lambda j: (j, 0, 0))],
        out_specs=(part, part),
        out_shape=(
            jax.ShapeDtypeStruct((rows, blocks * block), BF),
            pltpu.HBM((rows, blocks * block), F32),
        ),
        compiler_params=params(),
        name="shared_in",
    )(*pieces, far(w))


def paired_act(kept, came, block=256):
    pre = kept + came.astype(F32)
    half = block // 2
    return jnp.concatenate(
        [
            silu_mul(pre[:, j : j + half], pre[:, j + half : j + block])
            for j in range(0, pre.shape[1], block)
        ],
        axis=1,
    )


def out_kernel(kept, came, w, act_out, *outs):
    act = paired_act(kept[...], came[...])
    act_out[...] = act
    rows = outs[0].shape[0]
    first = act.shape[0] - rows * len(outs)
    total = dot(act[first:, :], w[...])
    for i, out in enumerate(outs):
        out[...] = total[i * rows : (i + 1) * rows].astype(BF)


def shared_out_part(kept, came, w, count, rows):
    units, width = w.shape
    return pl.pallas_call(
        out_kernel,
        in_specs=[pl.BlockSpec(memory_space=pltpu.VMEM)] * 3,
        out_shape=(jax.ShapeDtypeStruct((kept.shape[0], units), BF),)
        + (jax.ShapeDtypeStruct((rows, width), BF),) * count,
        compiler_params=params(),
        name="shared_out",
    )(kept, came, w)


def base_kernel(act, w, a, b, c, out):
    total = dot(act[...], w[...])
    out[...] = total + a[...].astype(F32) + b[...].astype(F32) + c[...].astype(F32)


def shared_sum(act, w, a, b, c, block=768):
    units, width = w.shape
    tokens = a.shape[0]
    part = pl.BlockSpec((tokens, block), lambda j: (0, j))
    return pl.pallas_call(
        base_kernel,
        grid=(width // block,),
        in_specs=[
            pl.BlockSpec((tokens, units), lambda j: (0, 0)),
            pl.BlockSpec((units, block), lambda j: (0, j)),
        ]
        + [part] * 3,
        out_specs=part,
        out_shape=pltpu.HBM((tokens, width), F32),
        compiler_params=params(),
        name="shared_sum",
    )(*(far(x) for x in (act, w, a, b, c)))


def turn_kernel(high, low, out):
    lanes, tokens = high.shape
    side = iota((tokens, lanes), 1) % (2 * CAP) // CAP
    for i, gates in enumerate((high, low)):
        turned = gates[...].astype(F32).T
        for h in range(2):
            out[h, i * tokens : (i + 1) * tokens, :] = jnp.where(side == h, turned, 0.0).astype(BF)


def turn_gates(high, low):
    lanes, tokens = high.shape
    return pl.pallas_call(
        turn_kernel,
        grid=(1,),
        out_shape=pltpu.HBM((2, 2 * tokens, lanes), BF),
        compiler_params=params(),
        name="turn_gates",
    )(high, low)


def mix_kernel(gates, back, base, out):
    tokens = out.shape[0]
    both = dot(gates[0], back[...])
    out[...] = (base[...] + both[:tokens] + both[tokens:]).astype(BF)


def mix(gates, back, base, block=768):
    _, both, lanes = gates.shape
    tokens, width = base.shape
    blocks = width // 2 // block
    part = pl.BlockSpec((tokens, block), lambda j: (0, j))
    return pl.pallas_call(
        mix_kernel,
        grid=(2 * blocks,),
        in_specs=[
            pl.BlockSpec((1, both, lanes), lambda j: (j // blocks, 0, 0)),
            pl.BlockSpec((lanes, block), lambda j: (0, j % blocks)),
            part,
        ],
        out_specs=part,
        out_shape=jax.ShapeDtypeStruct((tokens, width), BF),
        compiler_params=params(),
        name="mix",
    )(far(gates), back, far(base))


def shift(array, axis, by):
    size = lax.axis_size(axis)
    return lax.ppermute(array, axis, [(i, (i + by) % size) for i in range(size)])


def exchange(rows):
    return lax.all_to_all(rows, ("dp", "expert"), split_axis=0, concat_axis=0, tiled=True)


def shards(
    hidden, expert_ids, gate_fixed, slot_expert, expert_in, expert_out, shared_in, shared_out
):
    tokens, width = hidden.shape
    slots = slot_expert.shape[0]
    half = width // 2
    me = lax.axis_index("tensor").astype(jnp.int32)[None]

    prev = shift(hidden, "dp", 1)
    nxt = shift(hidden, "dp", -1)
    send_rows, high, low = route(expert_ids, gate_fixed, slot_expert, hidden)
    arrived = exchange(send_rows.reshape(slots, 2 * CAP, half))
    arrived = arrived.reshape(-1, half)
    w_in = []
    for part in range(2):
        w_in.append(split_gate_up(expert_in[0], 256, False, part, 2))
    w_shared = split_gate_up(shared_in, 256, True, depth=1024)
    n_sent, n_kept = shared_in_part((hidden, prev, nxt), w_shared)
    n_came = shift(n_sent, "tensor", 1)
    opposite = shift(hidden, "dp", 2)

    x, sent = send_half(arrived, w_in, me)
    came = shift(sent, "tensor", 1)
    kept = keep_half(x, w_in, me)
    own_act, down, up = shared_out_part(n_kept, n_came, shared_out, 2, tokens)
    from_prev = shift(up, "dp", 1)
    from_next = shift(down, "dp", -1)
    f_sent, f_kept = shared_in_part((opposite,), w_shared)
    f_came = shift(f_sent, "tensor", 1)

    act = activate(kept, came)
    act_other = shift(act, "tensor", 1)
    _, far_part = shared_out_part(f_kept, f_came, shared_out, 1, tokens)
    from_far = shift(far_part, "dp", 2)

    rows = answers(act, act_other, expert_out[0], me)
    back = exchange(rows.reshape(slots, 2 * CAP, half))
    back = back.reshape(-1, half)
    gates = turn_gates(high, low)
    base = shared_sum(own_act, shared_out, from_prev, from_next, from_far)
    return mix(gates, back, base)


def solution(mesh):
    in_specs = (
        P(("dp", "expert"), "tensor"),
        P(("dp", "expert"), None),
        P(("dp", "expert"), None),
        P(),
        P(("dp", "expert"), "tensor", None, None),
        P(("dp", "expert"), None, "tensor"),
        P("tensor", None, "dp"),
        P("dp", "tensor"),
    )
    out_specs = P(("dp", "expert"), "tensor")
    return jax.shard_map(shards, mesh=mesh, in_specs=in_specs, out_specs=out_specs, check_vma=False)
```

profile of v0, /device:TPU:1, one launch (start us, length us, event | category | flops | bytes accessed | tf_op | source)
XLA Modules:
  0.0 159.8 jit_solution(11509397555641507724)
XLA Ops:
  0.0 4.8 %route.1 = (bf16[512,1536]{1,0:T(8,128)(2,1)}, bf16[512,128]{1,0:T(8,128)(2,1)}, bf16[512,128]{1,0:T(8,128)(2,1)}) custom-call(s32[8,128]{1,0:T(8,128)} %bitcast.20, s32[8,128]{1,0:T(8,128)} %bitcast.21, s32[1,64]{1,0:T(1,128)} %bitcast.22, bf16[128,3072]{1,0:T(8,128)(2,1)} %refs_0_.1, bf16[128,3072]{1,0:T(8,128)(2,1)} %refs_0_.1), custom_call_target="tpu_custom_call" | custom-call | tf_op jit(solution)/shard_map/route/pallas_call | solution.py:80
  4.8 12.5 %all-to-all-start = ((bf16[64,8,1536]{2,1,0:T(8,128)(2,1)}), bf16[64,8,1536]{2,1,0:T(8,128)(2,1)S(1)}, u32[]{:S(2)}, u32[]{:S(2)}) async-start(bf16[64,8,1536]{2,1,0:T(8,128)(2,1)} %bitcast.19), calls=%async_computation | async-start | bytes 3145728 | tf_op jit(solution)/shard_map/all_to_all | solution.py:423
  17.3 7.5 %split.3.w_left = bf16[8,1536,256]{2,1,0:T(8,128)(2,1)} custom-call(bf16[3072,2,1024]{2,1,0:T(2,128)(2,1)} %bitcast.16), custom_call_target="tpu_custom_call" | custom-call | tf_op jit(solution)/shard_map/split/pallas_call | solution.py:132
  24.8 7.6 %split.4.w_right = bf16[8,1536,256]{2,1,0:T(8,128)(2,1)} custom-call(bf16[3072,2,1024]{2,1,0:T(2,128)(2,1)} %bitcast.17), custom_call_target="tpu_custom_call" | custom-call | tf_op jit(solution)/shard_map/split/pallas_call | solution.py:132
  32.4 10.4 %all-to-all-done = bf16[64,8,1536]{2,1,0:T(8,128)(2,1)S(1)} async-done(((bf16[64,8,1536]{2,1,0:T(8,128)(2,1)}), bf16[64,8,1536]{2,1,0:T(8,128)(2,1)S(1)}, u32[]{:S(2)}, u32[]{:S(2)}) %all-to-all-start) | async-done | bytes 1572896 | tf_op jit(solution)/shard_map/all_to_all | solution.py:423
  42.8 5.8 %send_half.1 = (bf16[256,3072]{1,0:T(8,128)(2,1)S(1)}, bf16[256,1024]{1,0:T(8,128)(2,1)S(1)}) custom-call(s32[1]{0:T(128)} %bitcast.3.me, bf16[512,1536]{1,0:T(8,128)(2,1)S(1)} %bitcast.11, bf16[8,1536,256]{2,1,0:T(8,128)(2,1)} %split.3.w_left, bf16[8,1536,256]{2,1,0:T(8,128)(2,1)} %split.4.w_right), custom_call_target="tpu_custom_call" | custom-call | tf_op jit(solution)/shard_map/send_half/pallas_call | solution.py:171
  48.6 0.4 collective-permute-start
  48.9 0.0 copy-done.1
  48.9 0.4 collective-permute-start.2
  49.3 2.3 %collective-permute-start.3 = (bf16[128,3072]{1,0:T(8,128)(2,1)S(1)}, bf16[128,3072]{1,0:T(8,128)(2,1)}, u32[]{:S(2)}, u32[]{:S(2)}) collective-permute-start(bf16[128,3072]{1,0:T(8,128)(2,1)S(1)} %copy-done.1), channel_id=1, source_target_pairs={{0,96},{32,0},{64,32},{96,64},{1,97},{33,1},{65,33},{97,65},{2,98}... | collective-permute-start | bytes 2359304 | tf_op jit(solution)/shard_map/ppermute | solution.py:419
  51.6 4.7 %keep_half.1.kept = f32[256,1024]{1,0:T(8,128)S(1)} custom-call(s32[1]{0:T(128)} %bitcast.3.me, bf16[256,3072]{1,0:T(8,128)(2,1)S(1)} %get-tuple-element.21.x, bf16[8,1536,256]{2,1,0:T(8,128)(2,1)} %split.3.w_left, bf16[8,1536,256]{2,1,0:T(8,128)(2,1)} %split.4.w_right), custom_call_target="tpu_custom_call" | custom-call | tf_op jit(solution)/shard_map/keep_half/pallas_call | solution.py:208
  56.3 5.4 %collective-permute-done.came = bf16[256,1024]{1,0:T(8,128)(2,1)S(1)} collective-permute-done((bf16[256,1024]{1,0:T(8,128)(2,1)S(1)}, bf16[256,1024]{1,0:T(8,128)(2,1)S(1)}, u32[]{:S(2)}, u32[]{:S(2)}) %collective-permute-start) | collective-permute-done | bytes 524320 | tf_op jit(solution)/shard_map/ppermute | solution.py:419
  61.7 0.2 activate.1.mine
  61.9 0.4 collective-permute-start.1
  62.2 0.0 collective-permute-start.7
  62.2 6.4 %collective-permute-done.1.other = bf16[256,512]{1,0:T(8,128)(2,1)S(1)} collective-permute-done((bf16[256,512]{1,0:T(8,128)(2,1)S(1)}, bf16[256,512]{1,0:T(8,128)(2,1)S(1)}, u32[]{:S(2)}, u32[]{:S(2)}) %collective-permute-start.1) | collective-permute-done | bytes 262176 | tf_op jit(solution)/shard_map/ppermute | solution.py:419
  68.6 6.3 %answers.1 = bf16[512,1536]{1,0:T(8,128)(2,1)} custom-call(s32[1]{0:T(128)} %bitcast.3.me, bf16[256,512]{1,0:T(8,128)(2,1)S(1)} %activate.1.mine, bf16[256,512]{1,0:T(8,128)(2,1)S(1)} %collective-permute-done.1.other, bf16[1024,3072]{1,0:T(8,128)(2,1)} %bitcast.12, bf16[1024,3072]{1,0:T(8,128)(2,1)} %bitcast.13, bf16[1024,3072]{1,0:T(8,128)(2,1)} %bitcast.14, ...), custom_call_target="tpu_custom_call" | custom-call | tf_op jit(solution)/shard_map/answers/pallas_call | solution.py:269
  75.0 6.5 %all-to-all-start.1 = ((bf16[64,8,1536]{2,1,0:T(8,128)(2,1)}), bf16[64,8,1536]{2,1,0:T(8,128)(2,1)S(1)}, u32[]{:S(2)}, u32[]{:S(2)}) async-start(bf16[64,8,1536]{2,1,0:T(8,128)(2,1)} %bitcast.18), calls=%async_computation.1 | async-start | bytes 3145728 | tf_op jit(solution)/shard_map/all_to_all | solution.py:423
  81.5 5.2 %split.5.refs_3_.refs_1_ = bf16[2,3072,256]{2,1,0:T(8,128)(2,1)} custom-call(bf16[3072,2,256]{2,1,0:T(2,128)(2,1)} %w.4), custom_call_target="tpu_custom_call" | custom-call | tf_op jit(solution)/shard_map/split/pallas_call | solution.py:132
  86.6 0.0 collective-permute-done.2.refs_1_
  86.6 0.0 collective-permute-done.3.refs_2_
  86.7 4.0 %shared_in.2 = (bf16[384,512]{1,0:T(8,128)(2,1)S(1)}, f32[384,512]{1,0:T(8,128)}) custom-call(bf16[128,3072]{1,0:T(8,128)(2,1)S(1)} %copy-done.1, bf16[128,3072]{1,0:T(8,128)(2,1)S(1)} %collective-permute-done.2.refs_1_, bf16[128,3072]{1,0:T(8,128)(2,1)} %collective-permute-done.3.refs_2_, bf16[2,3072,256]{2,1,0:T(8,128)(2,1)} %split.5.refs_3_.refs_1_), custom_call_target="tpu_custom_call" | custom-call | tf_op jit(solution)/shard_map/shared_in/pallas_call | solution.py:298
  90.6 0.3 collective-permute-start.4
  90.9 0.0 collective-permute-done.7.refs_0_
  91.0 3.3 %shared_in.3 = (bf16[128,512]{1,0:T(8,128)(2,1)S(1)}, f32[128,512]{1,0:T(8,128)}) custom-call(bf16[128,3072]{1,0:T(8,128)(2,1)} %collective-permute-done.7.refs_0_, bf16[2,3072,256]{2,1,0:T(8,128)(2,1)} %split.5.refs_3_.refs_1_), custom_call_target="tpu_custom_call" | custom-call | tf_op jit(solution)/shard_map/shared_in/pallas_call | solution.py:298
  94.3 1.0 collective-permute-start.8
  95.3 10.0 %collective-permute-done.8.came = bf16[128,512]{1,0:T(8,128)(2,1)S(1)} collective-permute-done((bf16[128,512]{1,0:T(8,128)(2,1)S(1)}, bf16[128,512]{1,0:T(8,128)(2,1)S(1)}, u32[]{:S(2)}, u32[]{:S(2)}) %collective-permute-start.8) | collective-permute-done | bytes 131104 | tf_op jit(solution)/shard_map/ppermute | solution.py:419
  105.3 0.0 copy-done
  105.3 0.9 copy-done.3
  106.3 0.7 shared_out.3
  107.0 8.0 %collective-permute-start.9 = (bf16[128,3072]{1,0:T(8,128)(2,1)S(1)}, bf16[128,3072]{1,0:T(8,128)(2,1)S(1)}, u32[]{:S(2)}, u32[]{:S(2)}) collective-permute-start(bf16[128,3072]{1,0:T(8,128)(2,1)S(1)} %get-tuple-element.30), channel_id=1, source_target_pairs={{0,64},{32,96},{64,0},{96,32},{1,65},{33,97},{65,1},{97,33},{2,66}... | collective-permute-start | bytes 2359304 | tf_op jit(solution)/shard_map/ppermute | solution.py:419
  115.0 0.0 collective-permute-done.4.came
  115.0 0.0 copy-done.2
  115.0 0.6 shared_out.2
  115.7 0.0 copy-start.4
  115.7 0.1 collective-permute-start.5
  115.8 2.7 %collective-permute-start.6 = (bf16[128,3072]{1,0:T(8,128)(2,1)S(1)}, bf16[128,3072]{1,0:T(8,128)(2,1)S(1)}, u32[]{:S(2)}, u32[]{:S(2)}) collective-permute-start(bf16[128,3072]{1,0:T(8,128)(2,1)S(1)} %get-tuple-element.27), channel_id=1, source_target_pairs={{0,96},{32,0},{64,32},{96,64},{1,97},{33,1},{65,33},{97,65},{2,98}... | collective-permute-start | bytes 2359304 | tf_op jit(solution)/shard_map/ppermute | solution.py:419
  118.4 0.0 copy-done.5
  118.4 0.9 turn_gates.1.gates
  119.4 10.9 %collective-permute-done.9.c = bf16[128,3072]{1,0:T(8,128)(2,1)S(1)} collective-permute-done((bf16[128,3072]{1,0:T(8,128)(2,1)S(1)}, bf16[128,3072]{1,0:T(8,128)(2,1)S(1)}, u32[]{:S(2)}, u32[]{:S(2)}) %collective-permute-start.9) | collective-permute-done | bytes 786464 | tf_op jit(solution)/shard_map/ppermute | solution.py:419
  130.3 19.6 %collective-permute-done.5.a = bf16[128,3072]{1,0:T(8,128)(2,1)S(1)} collective-permute-done((bf16[128,3072]{1,0:T(8,128)(2,1)S(1)}, bf16[128,3072]{1,0:T(8,128)(2,1)S(1)}, u32[]{:S(2)}, u32[]{:S(2)}) %collective-permute-start.5) | collective-permute-done | bytes 786464 | tf_op jit(solution)/shard_map/ppermute | solution.py:419
  149.9 0.0 collective-permute-done.6.b
  149.9 0.0 copy-done.4
  149.9 0.9 copy-done.8
  150.7 0.3 copy-done.9
  151.0 4.5 %shared_sum.1.base = f32[128,3072]{1,0:T(8,128)} custom-call(bf16[384,256]{1,0:T(8,128)(2,1)} %copy-done.4, bf16[256,3072]{1,0:T(8,128)(2,1)} %w.7, bf16[128,3072]{1,0:T(8,128)(2,1)} %copy-done.8, bf16[128,3072]{1,0:T(8,128)(2,1)} %copy-done.9, bf16[128,3072]{1,0:T(8,128)(2,1)} %copy-done.7), custom_call_target="tpu_custom_call" | custom-call | tf_op jit(solution)/shard_map/shared_sum/pallas_call | solution.py:356
  155.5 0.0 all-to-all-done.1
  155.5 4.3 %mix.1 = bf16[128,3072]{1,0:T(8,128)(2,1)} custom-call(bf16[2,256,512]{2,1,0:T(8,128)(2,1)} %turn_gates.1.gates, bf16[512,1536]{1,0:T(8,128)(2,1)S(1)} %bitcast.10, f32[128,3072]{1,0:T(8,128)} %shared_sum.1.base), custom_call_target="tpu_custom_call" | custom-call | tf_op jit(solution)/shard_map/mix/pallas_call | solution.py:402
  (11 shorter events, 0.0 us)
Async XLA Ops:
  4.8 37.9 %all-to-all-start = ((bf16[64,8,1536]{2,1,0:T(8,128)(2,1)}), bf16[64,8,1536]{2,1,0:T(8,128)(2,1)S(1)}, u32[]{:S(2)}, u32[]{:S(2)}) async-start(bf16[64,8,1536]{2,1,0:T(8,128)(2,1)} %bitcast.19), calls=%async_computation | async-start | bytes 3145728 | tf_op jit(solution)/shard_map/all_to_all | solution.py:423
  42.8 6.2 %copy-start.1 = (bf16[128,3072]{1,0:T(8,128)(2,1)S(1)}, bf16[128,3072]{1,0:T(8,128)(2,1)}, u32[]{:S(2)}) copy-start(bf16[128,3072]{1,0:T(8,128)(2,1)} %refs_0_.1) | copy-start | bytes 2359300
  48.6 13.2 %collective-permute-start = (bf16[256,1024]{1,0:T(8,128)(2,1)S(1)}, bf16[256,1024]{1,0:T(8,128)(2,1)S(1)}, u32[]{:S(2)}, u32[]{:S(2)}) collective-permute-start(bf16[256,1024]{1,0:T(8,128)(2,1)S(1)} %get-tuple-element.22), channel_id=1, source_target_pairs={{0,1},{1,0},{2,3},{3,2},{4,5},{5,4},{6,7},{7,6},{8,9},{9,8},{10,11... | collective-permute-start | bytes 1572872 | tf_op jit(solution)/shard_map/ppermute | solution.py:419
  48.9 37.7 %collective-permute-start.2 = (bf16[128,3072]{1,0:T(8,128)(2,1)S(1)}, bf16[128,3072]{1,0:T(8,128)(2,1)S(1)}, u32[]{:S(2)}, u32[]{:S(2)}) collective-permute-start(bf16[128,3072]{1,0:T(8,128)(2,1)S(1)} %copy-done.1), channel_id=1, source_target_pairs={{0,32},{32,64},{64,96},{96,0},{1,33},{33,65},{65,97},{97,1},{2,34}... | collective-permute-start | bytes 2359304 | tf_op jit(solution)/shard_map/ppermute | solution.py:419
  49.3 37.3 %collective-permute-start.3 = (bf16[128,3072]{1,0:T(8,128)(2,1)S(1)}, bf16[128,3072]{1,0:T(8,128)(2,1)}, u32[]{:S(2)}, u32[]{:S(2)}) collective-permute-start(bf16[128,3072]{1,0:T(8,128)(2,1)S(1)} %copy-done.1), channel_id=1, source_target_pairs={{0,96},{32,0},{64,32},{96,64},{1,97},{33,1},{65,33},{97,65},{2,98}... | collective-permute-start | bytes 2359304 | tf_op jit(solution)/shard_map/ppermute | solution.py:419
  61.9 6.8 %collective-permute-start.1 = (bf16[256,512]{1,0:T(8,128)(2,1)S(1)}, bf16[256,512]{1,0:T(8,128)(2,1)S(1)}, u32[]{:S(2)}, u32[]{:S(2)}) collective-permute-start(bf16[256,512]{1,0:T(8,128)(2,1)S(1)} %activate.1.mine), channel_id=1, source_target_pairs={{0,1},{1,0},{2,3},{3,2},{4,5},{5,4},{6,7},{7,6},{8,9},{9,8},{10,11... | collective-permute-start | bytes 786440 | tf_op jit(solution)/shard_map/ppermute | solution.py:419
  62.2 28.7 %collective-permute-start.7 = (bf16[128,3072]{1,0:T(8,128)(2,1)S(1)}, bf16[128,3072]{1,0:T(8,128)(2,1)}, u32[]{:S(2)}, u32[]{:S(2)}) collective-permute-start(bf16[128,3072]{1,0:T(8,128)(2,1)S(1)} %copy-done.1), channel_id=1, source_target_pairs={{0,64},{32,96},{64,0},{96,32},{1,65},{33,97},{65,1},{97,33},{2,66}... | collective-permute-start | bytes 2359304 | tf_op jit(solution)/shard_map/ppermute | solution.py:419
  75.0 80.6 %all-to-all-start.1 = ((bf16[64,8,1536]{2,1,0:T(8,128)(2,1)}), bf16[64,8,1536]{2,1,0:T(8,128)(2,1)S(1)}, u32[]{:S(2)}, u32[]{:S(2)}) async-start(bf16[64,8,1536]{2,1,0:T(8,128)(2,1)} %bitcast.18), calls=%async_computation.1 | async-start | bytes 3145728 | tf_op jit(solution)/shard_map/all_to_all | solution.py:423
  90.6 14.7 %copy-start = (bf16[256,3072]{1,0:T(8,128)(2,1)S(1)}, bf16[256,3072]{1,0:T(8,128)(2,1)}, u32[]{:S(2)}) copy-start(bf16[256,3072]{1,0:T(8,128)(2,1)} %w.7) | copy-start | bytes 4718596
  90.6 24.4 %collective-permute-start.4 = (bf16[384,512]{1,0:T(8,128)(2,1)S(1)}, bf16[384,512]{1,0:T(8,128)(2,1)S(1)}, u32[]{:S(2)}, u32[]{:S(2)}) collective-permute-start(bf16[384,512]{1,0:T(8,128)(2,1)S(1)} %get-tuple-element.24), channel_id=1, source_target_pairs={{0,1},{1,0},{2,3},{3,2},{4,5},{5,4},{6,7},{7,6},{8,9},{9,8},{10,11... | collective-permute-start | bytes 1179656 | tf_op jit(solution)/shard_map/ppermute | solution.py:419
  94.3 20.7 %copy-start.2 = (f32[384,512]{1,0:T(8,128)S(1)}, f32[384,512]{1,0:T(8,128)}, u32[]{:S(2)}) copy-start(f32[384,512]{1,0:T(8,128)} %get-tuple-element.23.kept) | copy-start | bytes 2359300
  94.3 11.0 %collective-permute-start.8 = (bf16[128,512]{1,0:T(8,128)(2,1)S(1)}, bf16[128,512]{1,0:T(8,128)(2,1)S(1)}, u32[]{:S(2)}, u32[]{:S(2)}) collective-permute-start(bf16[128,512]{1,0:T(8,128)(2,1)S(1)} %get-tuple-element.29), channel_id=1, source_target_pairs={{0,1},{1,0},{2,3},{3,2},{4,5},{5,4},{6,7},{7,6},{8,9},{9,8},{10,11... | collective-permute-start | bytes 393224 | tf_op jit(solution)/shard_map/ppermute | solution.py:419
  105.3 1.0 copy-start.3
  107.0 11.4 %copy-start.5 = (bf16[512,128]{1,0:T(8,128)(2,1)S(1)}, bf16[512,128]{1,0:T(8,128)(2,1)}, u32[]{:S(2)}) copy-start(bf16[512,128]{1,0:T(8,128)(2,1)} %get-tuple-element.18.high) | copy-start | bytes 393220
  107.0 11.4 %copy-start.6 = (bf16[512,128]{1,0:T(8,128)(2,1)S(1)}, bf16[512,128]{1,0:T(8,128)(2,1)}, u32[]{:S(2)}) copy-start(bf16[512,128]{1,0:T(8,128)(2,1)} %get-tuple-element.19.low) | copy-start | bytes 393220
  107.0 23.3 %collective-permute-start.9 = (bf16[128,3072]{1,0:T(8,128)(2,1)S(1)}, bf16[128,3072]{1,0:T(8,128)(2,1)S(1)}, u32[]{:S(2)}, u32[]{:S(2)}) collective-permute-start(bf16[128,3072]{1,0:T(8,128)(2,1)S(1)} %get-tuple-element.30), channel_id=1, source_target_pairs={{0,64},{32,96},{64,0},{96,32},{1,65},{33,97},{65,1},{97,33},{2,66}... | collective-permute-start | bytes 2359304 | tf_op jit(solution)/shard_map/ppermute | solution.py:419
  115.7 34.2 %copy-start.4 = (bf16[384,256]{1,0:T(8,128)(2,1)}, bf16[384,256]{1,0:T(8,128)(2,1)S(1)}, u32[]{:S(2)}) copy-start(bf16[384,256]{1,0:T(8,128)(2,1)S(1)} %get-tuple-element.25.act) | copy-start | bytes 589828
  115.7 34.2 %collective-permute-start.5 = (bf16[128,3072]{1,0:T(8,128)(2,1)S(1)}, bf16[128,3072]{1,0:T(8,128)(2,1)S(1)}, u32[]{:S(2)}, u32[]{:S(2)}) collective-permute-start(bf16[128,3072]{1,0:T(8,128)(2,1)S(1)} %get-tuple-element.26), channel_id=1, source_target_pairs={{0,32},{32,64},{64,96},{96,0},{1,33},{33,65},{65,97},{97,1},{2,34}... | collective-permute-start | bytes 2359304 | tf_op jit(solution)/shard_map/ppermute | solution.py:419
  115.8 34.1 %collective-permute-start.6 = (bf16[128,3072]{1,0:T(8,128)(2,1)S(1)}, bf16[128,3072]{1,0:T(8,128)(2,1)S(1)}, u32[]{:S(2)}, u32[]{:S(2)}) collective-permute-start(bf16[128,3072]{1,0:T(8,128)(2,1)S(1)} %get-tuple-element.27), channel_id=1, source_target_pairs={{0,96},{32,0},{64,32},{96,64},{1,97},{33,1},{65,33},{97,65},{2,98}... | collective-permute-start | bytes 2359304 | tf_op jit(solution)/shard_map/ppermute | solution.py:419
  130.3 19.6 %copy-start.7 = (bf16[128,3072]{1,0:T(8,128)(2,1)}, bf16[128,3072]{1,0:T(8,128)(2,1)S(1)}, u32[]{:S(2)}) copy-start(bf16[128,3072]{1,0:T(8,128)(2,1)S(1)} %collective-permute-done.9.c) | copy-start | bytes 2359300
  149.9 0.9 copy-start.8
  149.9 1.2 copy-start.9
where the time goes:
time: 161 us; the launch traced here: 160 us
  waiting for transfers between devices  62.7 us (39%)
  Pallas kernels  60.5 us (38%)
  starting transfers between devices  34.5 us (21%)
  local copies, waits for them, and re-layouts  2.12 us (1%)
    ppermute x10, waiting for transfers between devices, shift(): lax.ppermute(array, axis, [(i, (i + by) % size) for i in range(size)])  52.3 us
    pallas_call x3, Pallas kernels, split_gate_up(): pl.pallas_call(functools.partial(split_kernel, sub=sub, paired=paired), g...  20.3 us
    all_to_all x2, starting transfers between devices, exchange(): lax.all_to_all(rows, ('dp', 'expert'), split_axis=0, concat_axis=0, tiled...  18.9 us
    ppermute x10, starting transfers between devices, shift(): lax.ppermute(array, axis, [(i, (i + by) % size) for i in range(size)])  15.5 us
    all_to_all x2, waiting for transfers between devices, exchange(): lax.all_to_all(rows, ('dp', 'expert'), split_axis=0, concat_axis=0, tiled...  10.4 us
    pallas_call x2, Pallas kernels, shared_in_part(): pl.pallas_call(shared_kernel, grid=(blocks,), in_specs=[pl.BlockSpec(memo...  7.32 us
    pallas_call x1, Pallas kernels, answers(): pl.pallas_call(answer_kernel, grid_spec=pltpu.PrefetchScalarGridSpec(num_...  6.32 us
    pallas_call x1, Pallas kernels, send_half(): pl.pallas_call(unfold_kernel, grid_spec=pltpu.PrefetchScalarGridSpec(num_...  5.78 us
  transfers between devices with their start and end apart: 12, of which 6 were waited for; matrix products, arithmetic and copies ran while one was open for 0% of the time, Pallas kernels for 29%

commit v1 on v0

v1 whole, which is shorter than its diff:
```python
import functools

import jax
import jax.numpy as jnp
from jax import lax
from jax.experimental import pallas as pl
from jax.experimental.pallas import tpu as pltpu
from jax.sharding import PartitionSpec as P


CAP = 4
BF = jnp.bfloat16
F32 = jnp.float32


def params(mib=20):
    return pltpu.CompilerParams(vmem_limit_bytes=mib * 2**20)


def far(array):
    return pltpu.with_memory_space_constraint(array, pltpu.HBM)


def dot(a, b):
    return jnp.dot(a, b, preferred_element_type=F32)


def iota(shape, dim):
    return lax.broadcasted_iota(jnp.int32, shape, dim)


def silu_mul(gate, up):
    return (jax.nn.silu(gate) * up).astype(BF)


def served_lanes(ids, held_row):
    slots = held_row.shape[1]
    lanes = slots * 2 * CAP
    tokens = ids.shape[1]
    col, slot = iota((lanes, slots), 1), iota((lanes, slots), 0) >> 3
    held_all = jnp.broadcast_to(held_row[...], (lanes, slots))
    held = jnp.max(jnp.where(col == slot, held_all, -1), axis=1, keepdims=True)
    twin = (held_all == held) & (col < slot)
    spare = jnp.max(jnp.where(twin, CAP, 0), axis=1, keepdims=True)
    named = jnp.zeros((lanes, tokens), F32)
    for k in range(ids.shape[0]):
        named = jnp.where(ids[k : k + 1, :] == held, 1.0, named)
    earlier = iota((tokens, tokens), 0) < iota((tokens, tokens), 1)
    rank = dot(named.astype(BF), jnp.where(earlier, 1.0, 0.0).astype(BF))
    row = iota((lanes, 1), 0)
    place = (spare + (row & (CAP - 1))).astype(F32)
    served = (named > 0.5) & (rank == place)
    return served, held, (row & CAP) == 0


def route_kernel(ids, held_row, left, right, rows_out, pick):
    @pl.when(pl.program_id(0) == 0)
    def _():
        served, _, is_left = served_lanes(ids, held_row)
        one = jnp.where(served, 1.0, 0.0)
        pick[0] = jnp.where(is_left, one, 0.0).astype(BF)
        pick[1] = jnp.where(is_left, 0.0, one).astype(BF)

    rows_out[...] = (dot(pick[0], left[...]) + dot(pick[1], right[...])).astype(BF)


def whole_of(array):
    return pl.BlockSpec(array.shape, lambda *_: (0,) * array.ndim)


def route(ids, slot_expert, hidden, block=768):
    slots = slot_expert.shape[0]
    lanes = slots * 2 * CAP
    tokens, width = hidden.shape
    half = width // 2
    blocks = half // block
    ids, held = ids.T, slot_expert[None]
    return pl.pallas_call(
        route_kernel,
        grid=(blocks,),
        in_specs=[
            whole_of(ids),
            whole_of(held),
            pl.BlockSpec((tokens, block), lambda j: (0, j)),
            pl.BlockSpec((tokens, block), lambda j: (0, blocks + j)),
        ],
        out_specs=pl.BlockSpec((lanes, block), lambda j: (0, j)),
        out_shape=pltpu.HBM((lanes, half), BF),
        scratch_shapes=[pltpu.VMEM((2, lanes, tokens), BF)],
        compiler_params=params(16),
        name="route",
    )(*(far(x) for x in (ids, held, hidden, hidden)))


def gates_kernel(ids, gates, held_row, out):
    served, held, is_left = served_lanes(ids, held_row)
    tokens = ids.shape[1]
    gate = jnp.zeros(served.shape, jnp.int32)
    for k in range(ids.shape[0]):
        gate = gate + jnp.where(ids[k : k + 1, :] == held, gates[k : k + 1, :], 0)
    gate = jnp.where(served, gate, 0)
    high = (gate >> 8).astype(F32) * 2.0**-8
    low = (gate & 255).astype(F32) * 2.0**-16
    for i, part in enumerate((high, low)):
        rows = slice(i * tokens, (i + 1) * tokens)
        out[0, rows, :] = jnp.where(is_left, part, 0.0).T.astype(BF)
        out[1, rows, :] = jnp.where(is_left, 0.0, part).T.astype(BF)


def combine_gates(ids, gates, slot_expert):
    lanes = slot_expert.shape[0] * 2 * CAP
    operands = ids.T, gates.T, slot_expert[None]
    shape = (2, 2 * ids.shape[0], lanes)
    return pl.pallas_call(
        gates_kernel,
        grid=(1,),
        in_specs=[whole_of(x) for x in operands],
        out_specs=pl.BlockSpec(shape, lambda j: (0, 0, 0)),
        out_shape=pltpu.HBM(shape, BF),
        compiler_params=params(16),
        name="combine_gates",
    )(*(far(x) for x in operands))


def split_kernel(w, w_shared, out, out_shared, *, sub):
    row, col = iota((2 * sub, 2 * sub), 0), iota((2 * sub, 2 * sub), 1)
    source = jnp.where(row < sub, 2 * row, 2 * (row - sub) + 1)
    order = jnp.where(col == source, 1.0, 0.0).astype(BF)
    block, part = out.shape[2], out_shared.shape[2] // 2
    for start in range(0, w.shape[0], sub):
        here = slice(start, start + sub)
        moved = dot(order, w[here].reshape(2 * sub, w.shape[2])).astype(BF)
        for j in range(2):
            cols = slice(j * block, (j + 1) * block)
            out[j, here, :] = moved[:sub, cols]
            out[2 + j, here, :] = moved[sub:, cols]
        moved = dot(order, w_shared[here].reshape(2 * sub, w_shared.shape[2])).astype(BF)
        for j in range(2):
            cols = slice(j * part, (j + 1) * part)
            out_shared[j, here, :part] = moved[:sub, cols]
            out_shared[j, here, part:] = moved[sub:, cols]


def split_gate_up(w, w_shared, depth=768, sub=128):
    width, _, units = w.shape
    shared_units = w_shared.shape[2]

    def taken(columns):
        return pl.BlockSpec((depth, 2, columns), lambda i: (i, 0, 0))

    def given(blocks, block):
        return pl.BlockSpec((blocks, depth, block), lambda i: (0, i, 0))

    return pl.pallas_call(
        functools.partial(split_kernel, sub=sub),
        grid=(width // depth,),
        in_specs=[taken(units), taken(shared_units)],
        out_specs=(given(4, units // 2), given(2, shared_units)),
        out_shape=(
            pltpu.HBM((4, width, units // 2), BF),
            pltpu.HBM((2, width, shared_units), BF),
        ),
        compiler_params=params(24),
        name="split",
    )(far(w), far(w_shared))


def fetch(w, held, sems, side):
    copies = []
    cut = w.shape[1] // 2
    for j in range(2):
        for k in range(2):
            rows = slice(k * cut, (k + 1) * cut)
            copies.append(
                pltpu.make_async_copy(
                    w.at[2 * j + side, rows], held.at[j, rows], sems.at[2 * j + k]
                )
            )
            copies[-1].start()
    return copies


def multiply(x, held, copies, out):
    cut, block = held.shape[1] // 2, held.shape[2]
    for j in range(2):
        total = None
        for k in range(2):
            copies[2 * j + k].wait()
            rows = slice(k * cut, (k + 1) * cut)
            part = dot(x[:, rows], held[j, rows])
            total = part if total is None else total + part
        out[:, j * block : (j + 1) * block] = total.astype(out.dtype)


def send_kernel(me, arrived, w, x_out, out, held, sems):
    copies = fetch(w, held, sems, 1 - me[0])
    half = arrived.shape[1]
    rows = arrived.shape[0] // 2
    row, col = iota((rows, 2 * rows), 0), iota((rows, 2 * rows), 1)
    first = ((row >> 2) << 3) + (row & 3)
    for h in range(2):
        pick = jnp.where(col == first + h * CAP, 1.0, 0.0).astype(BF)
        x_out[:, h * half : (h + 1) * half] = dot(pick, arrived[...]).astype(BF)
    multiply(x_out, held, copies, out)


def weight_scratch(w):
    return [pltpu.VMEM((2, *w.shape[1:]), BF), pltpu.SemaphoreType.DMA((4,))]


def send_half(arrived, w, me):
    lanes, half = arrived.shape
    rows, units = lanes // 2, 2 * w.shape[2]
    near = pl.BlockSpec(memory_space=pltpu.VMEM)
    return pl.pallas_call(
        send_kernel,
        in_specs=[pl.BlockSpec(memory_space=pltpu.SMEM), near, pl.BlockSpec(memory_space=pl.ANY)],
        out_shape=(
            jax.ShapeDtypeStruct((rows, 2 * half), BF),
            jax.ShapeDtypeStruct((rows, units), BF),
        ),
        scratch_shapes=weight_scratch(w),
        compiler_params=params(),
        name="send_half",
    )(me, arrived, far(w))


def keep_kernel(me, x, w, out, held, sems):
    multiply(x, held, fetch(w, held, sems, me[0]), out)


def keep_half(x, w, me):
    near = pl.BlockSpec(memory_space=pltpu.VMEM)
    return pl.pallas_call(
        keep_kernel,
        in_specs=[pl.BlockSpec(memory_space=pltpu.SMEM), near, pl.BlockSpec(memory_space=pl.ANY)],
        out_shape=jax.ShapeDtypeStruct((x.shape[0], 2 * w.shape[2]), F32),
        scratch_shapes=weight_scratch(w),
        compiler_params=params(),
        name="keep_half",
    )(me, x, far(w))


def act_kernel(kept, came, out):
    units = out.shape[1]
    pre = kept[...] + came[...].astype(F32)
    out[...] = silu_mul(pre[:, :units], pre[:, units:])


def activate(kept, came):
    rows, units = kept.shape
    return pl.pallas_call(
        act_kernel,
        out_shape=jax.ShapeDtypeStruct((rows, units // 2), BF),
        compiler_params=params(),
        name="activate",
    )(kept, came)


def answer_kernel(me, mine, other, w, out, *, block):
    rows, units = mine.shape
    half = out.shape[1]
    row, col = iota((2 * rows, rows), 0), iota((2 * rows, rows), 1)
    first = ((col >> 2) << 3) + (col & 3)
    place = [jnp.where(row == first + h * CAP, 1.0, 0.0).astype(BF) for h in range(2)]
    at_mine = pl.ds(pl.multiple_of(me[0] * units, units), units)
    at_other = pl.ds(pl.multiple_of((1 - me[0]) * units, units), units)

    def answer(start):
        cols = slice(start, start + block)
        return (dot(mine[...], w[at_mine, cols]) + dot(other[...], w[at_other, cols])).astype(BF)

    for start in range(0, half, block):
        total = dot(place[0], answer(start)) + dot(place[1], answer(half + start))
        out[:, start : start + block] = total.astype(BF)


def answers(mine, other, w, me, block=768):
    rows, _ = mine.shape
    near = pl.BlockSpec(memory_space=pltpu.VMEM)
    return pl.pallas_call(
        functools.partial(answer_kernel, block=block),
        in_specs=[pl.BlockSpec(memory_space=pltpu.SMEM)] + [near] * 3,
        out_shape=jax.ShapeDtypeStruct((2 * rows, w.shape[1] // 2), BF),
        compiler_params=params(),
        name="answers",
    )(me, mine, other, w)


def shared_kernel(*refs, count, ahead):
    pieces, w, sent, kept = refs[:count], *refs[count : count + 3]
    pre = dot(jnp.concatenate([piece[...] for piece in pieces], axis=0), w[0])
    sent[...] = pre.astype(BF)
    kept[...] = pre
    if ahead:

        @pl.when(pl.program_id(0) == 0)
        def _():
            up, down = refs[count + 3 :]
            rows = up.shape[0]
            up[...] = pieces[1][:rows, :]
            down[...] = pieces[2][rows:, :]


def shared_in_part(pieces, w, ahead):
    rows = sum(piece.shape[0] for piece in pieces)
    blocks, width, block = w.shape
    part = pl.BlockSpec((rows, block), lambda j: (0, j))
    out_specs = [part, part]
    out_shape = [
        jax.ShapeDtypeStruct((rows, blocks * block), BF),
        pltpu.HBM((rows, blocks * block), F32),
    ]
    if ahead:
        shape = (pieces[0].shape[0] // 2, width)
        out_specs += [pl.BlockSpec(shape, lambda j: (0, 0))] * 2
        out_shape += [jax.ShapeDtypeStruct(shape, BF)] * 2
    return pl.pallas_call(
        functools.partial(shared_kernel, count=len(pieces), ahead=ahead),
        grid=(blocks,),
        in_specs=[pl.BlockSpec(memory_space=pltpu.VMEM)] * len(pieces)
        + [pl.BlockSpec((1, width, block), lambda j: (j, 0, 0))],
        out_specs=tuple(out_specs),
        out_shape=tuple(out_shape),
        compiler_params=params(),
        name="shared_in",
    )(*pieces, far(w))


def paired_act(kept, came, block=256):
    pre = kept + came.astype(F32)
    half = block // 2
    return jnp.concatenate(
        [
            silu_mul(pre[:, j : j + half], pre[:, j + half : j + block])
            for j in range(0, pre.shape[1], block)
        ],
        axis=1,
    )


def out_kernel(kept, came, w, act_out, *outs):
    act = paired_act(kept[...], came[...])
    act_out[...] = act
    rows = outs[0].shape[0]
    first = act.shape[0] - rows * len(outs)
    total = dot(act[first:, :], w[...])
    for i, out in enumerate(outs):
        out[...] = total[i * rows : (i + 1) * rows].astype(BF)


def shared_out_part(kept, came, w, count, rows):
    units, width = w.shape
    return pl.pallas_call(
        out_kernel,
        in_specs=[pl.BlockSpec(memory_space=pltpu.VMEM)] * 3,
        out_shape=(jax.ShapeDtypeStruct((kept.shape[0], units), BF),)
        + (jax.ShapeDtypeStruct((rows, width), BF),) * count,
        compiler_params=params(),
        name="shared_out",
    )(kept, came, w)


def base_kernel(act, w, out):
    out[...] = dot(act[...], w[...])


def own_sum(act, w, tokens, block=1536):
    units, width = w.shape
    return pl.pallas_call(
        base_kernel,
        grid=(width // block,),
        in_specs=[
            pl.BlockSpec((tokens, units), lambda j: (0, 0)),
            pl.BlockSpec((units, block), lambda j: (0, j)),
        ],
        out_specs=pl.BlockSpec((tokens, block), lambda j: (0, j)),
        out_shape=pltpu.HBM((tokens, width), F32),
        compiler_params=params(),
        name="own_sum",
    )(far(act), far(w))


def mix_kernel(gates, back, base, a, b, c, out):
    tokens = out.shape[0]
    total = base[...] + a[...].astype(F32) + b[...].astype(F32) + c[...].astype(F32)
    both = dot(gates[0], back[...])
    out[...] = (total + both[:tokens] + both[tokens:]).astype(BF)


def mix(gates, back, base, came, block=1536):
    _, both, lanes = gates.shape
    tokens, width = base.shape
    blocks = width // 2 // block
    part = pl.BlockSpec((tokens, block), lambda j: (0, j))
    return pl.pallas_call(
        mix_kernel,
        grid=(2 * blocks,),
        in_specs=[
            pl.BlockSpec((1, both, lanes), lambda j: (j // blocks, 0, 0)),
            pl.BlockSpec((lanes, block), lambda j: (0, j % blocks)),
        ]
        + [part] * 4,
        out_specs=part,
        out_shape=jax.ShapeDtypeStruct((tokens, width), BF),
        compiler_params=params(),
        name="mix",
    )(far(gates), back, far(base), *(far(x) for x in came))


def shift(array, axis, by):
    size = lax.axis_size(axis)
    return lax.ppermute(array, axis, [(i, (i + by) % size) for i in range(size)])


def exchange(rows):
    return lax.all_to_all(rows, ("dp", "expert"), split_axis=0, concat_axis=0, tiled=True)


def shards(
    hidden, expert_ids, gate_fixed, slot_expert, expert_in, expert_out, shared_in, shared_out
):
    tokens, width = hidden.shape
    slots = slot_expert.shape[0]
    half = width // 2
    me = lax.axis_index("tensor").astype(jnp.int32)[None]

    prev = shift(hidden, "dp", 1)
    nxt = shift(hidden, "dp", -1)
    send_rows = route(expert_ids, slot_expert, hidden)
    arrived = exchange(send_rows.reshape(slots, 2 * CAP, half))
    arrived = arrived.reshape(-1, half)
    w_in, w_shared = split_gate_up(expert_in[0], shared_in)
    n_sent, n_kept, ahead, behind = shared_in_part((hidden, prev, nxt), w_shared, True)
    n_came = shift(n_sent, "tensor", 1)
    far_a = shift(ahead, "dp", 1)
    far_b = shift(behind, "dp", -1)

    x, sent = send_half(arrived, w_in, me)
    came = shift(sent, "tensor", 1)
    kept = keep_half(x, w_in, me)
    own_act, down, up = shared_out_part(n_kept, n_came, shared_out, 2, tokens)
    from_prev = shift(up, "dp", 1)
    from_next = shift(down, "dp", -1)
    f_sent, f_kept = shared_in_part((far_a, far_b), w_shared, False)
    f_came = shift(f_sent, "tensor", 1)

    act = activate(kept, came)
    act_other = shift(act, "tensor", 1)
    _, far_part = shared_out_part(f_kept, f_came, shared_out, 1, tokens)
    from_far = shift(far_part, "dp", 2)

    rows = answers(act, act_other, expert_out[0], me)
    back = exchange(rows.reshape(slots, 2 * CAP, half))
    back = back.reshape(-1, half)
    gates = combine_gates(expert_ids, gate_fixed, slot_expert)
    base = own_sum(own_act, shared_out, tokens)
    return mix(gates, back, base, (from_prev, from_next, from_far))


def solution(mesh):
    in_specs = (
        P(("dp", "expert"), "tensor"),
        P(("dp", "expert"), None),
        P(("dp", "expert"), None),
        P(),
        P(("dp", "expert"), "tensor", None, None),
        P(("dp", "expert"), None, "tensor"),
        P("tensor", None, "dp"),
        P("dp", "tensor"),
    )
    out_specs = P(("dp", "expert"), "tensor")
    return jax.shard_map(shards, mesh=mesh, in_specs=in_specs, out_specs=out_specs, check_vma=False)
```

time: 161 us -> 153 us (0.950)
  the two profiles are of different devices: /device:TPU:1 before, /device:TPU:4 now
where the time goes in v1:
time: 153 us; the launch traced here: 152 us
  waiting for transfers between devices  68.3 us (45%)
  Pallas kernels  46.1 us (30%)
  starting transfers between devices  36 us (24%)
  local copies, waits for them, and re-layouts  1.85 us (1%)
    ppermute x11, waiting for transfers between devices, shift(): lax.ppermute(array, axis, [(i, (i + by) % size) for i in range(size)])  58.5 us
    all_to_all x2, starting transfers between devices, exchange(): lax.all_to_all(rows, ('dp', 'expert'), split_axis=0, concat_axis=0, tiled...  21 us
    ppermute x11, starting transfers between devices, shift(): lax.ppermute(array, axis, [(i, (i + by) % size) for i in range(size)])  15.1 us
    pallas_call x1, Pallas kernels, split_gate_up(): pl.pallas_call(functools.partial(split_kernel, sub=sub), grid=(width // d...  12.9 us
    all_to_all x2, waiting for transfers between devices, exchange(): lax.all_to_all(rows, ('dp', 'expert'), split_axis=0, concat_axis=0, tiled...  9.76 us
    pallas_call x2, Pallas kernels, shared_in_part(): pl.pallas_call(functools.partial(shared_kernel, count=len(pieces), ahead=...  6.97 us
    pallas_call x1, Pallas kernels, keep_half(): pl.pallas_call(keep_kernel, in_specs=[pl.BlockSpec(memory_space=pltpu.SME...  4.17 us
    pallas_call x1, Pallas kernels, send_half(): pl.pallas_call(send_kernel, in_specs=[pl.BlockSpec(memory_space=pltpu.SME...  4.11 us
  transfers between devices with their start and end apart: 13, of which 5 were waited for; matrix products, arithmetic and copies ran while one was open for 0% of the time, Pallas kernels for 23%

profile of v1, /device:TPU:4, one launch (start us, length us, event | category | flops | bytes accessed | tf_op | source)
XLA Modules:
  0.0 152.3 jit_solution(9556053535652073856)
XLA Ops:
  0.0 3.7 %route.1 = bf16[512,1536]{1,0:T(8,128)(2,1)} custom-call(s32[8,128]{1,0:T(8,128)} %bitcast.17, s32[1,64]{1,0:T(1,128)} %bitcast.20, bf16[128,3072]{1,0:T(8,128)(2,1)} %refs_0_.1, bf16[128,3072]{1,0:T(8,128)(2,1)} %refs_0_.1), custom_call_target="tpu_custom_call" | custom-call | tf_op jit(solution)/shard_map/route/pallas_call | solution.py:78
  3.7 11.5 %all-to-all-start = ((bf16[64,8,1536]{2,1,0:T(8,128)(2,1)}), bf16[64,8,1536]{2,1,0:T(8,128)(2,1)S(1)}, u32[]{:S(2)}, u32[]{:S(2)}) async-start(bf16[64,8,1536]{2,1,0:T(8,128)(2,1)} %bitcast.16), calls=%async_computation | async-start | bytes 3145728 | tf_op jit(solution)/shard_map/all_to_all | solution.py:417
  15.2 12.9 %split.1 = (bf16[4,3072,512]{2,1,0:T(8,128)(2,1)}, bf16[2,3072,256]{2,1,0:T(8,128)(2,1)}) custom-call(bf16[3072,2,1024]{2,1,0:T(2,128)(2,1)} %bitcast.15, bf16[3072,2,256]{2,1,0:T(2,128)(2,1)} %w_shared.1), custom_call_target="tpu_custom_call" | custom-call | tf_op jit(solution)/shard_map/split/pallas_call | solution.py:154
  28.1 9.8 %all-to-all-done = bf16[64,8,1536]{2,1,0:T(8,128)(2,1)S(1)} async-done(((bf16[64,8,1536]{2,1,0:T(8,128)(2,1)}), bf16[64,8,1536]{2,1,0:T(8,128)(2,1)S(1)}, u32[]{:S(2)}, u32[]{:S(2)}) %all-to-all-start) | async-done | bytes 1572896 | tf_op jit(solution)/shard_map/all_to_all | solution.py:417
  37.9 4.1 %send_half.1 = (bf16[256,3072]{1,0:T(8,128)(2,1)S(1)}, bf16[256,1024]{1,0:T(8,128)(2,1)S(1)}) custom-call(s32[1]{0:T(128)} %bitcast.3.me, bf16[512,1536]{1,0:T(8,128)(2,1)S(1)} %bitcast.14, bf16[4,3072,512]{2,1,0:T(8,128)(2,1)} %get-tuple-element.19.w), custom_call_target="tpu_custom_call" | custom-call | tf_op jit(solution)/shard_map/send_half/pallas_call | solution.py:215
  42.0 1.3 collective-permute-start
  43.3 0.0 copy-done.1
  43.3 0.0 collective-permute-start.2
  43.3 3.2 %collective-permute-start.3 = (bf16[128,3072]{1,0:T(8,128)(2,1)S(1)}, bf16[128,3072]{1,0:T(8,128)(2,1)}, u32[]{:S(2)}, u32[]{:S(2)}) collective-permute-start(bf16[128,3072]{1,0:T(8,128)(2,1)S(1)} %copy-done.1), channel_id=1, source_target_pairs={{0,96},{32,0},{64,32},{96,64},{1,97},{33,1},{65,33},{97,65},{2,98}... | collective-permute-start | bytes 2359304 | tf_op jit(solution)/shard_map/ppermute | solution.py:413
  46.5 4.2 %keep_half.1.kept = f32[256,1024]{1,0:T(8,128)S(1)} custom-call(s32[1]{0:T(128)} %bitcast.3.me, bf16[256,3072]{1,0:T(8,128)(2,1)S(1)} %get-tuple-element.20.x, bf16[4,3072,512]{2,1,0:T(8,128)(2,1)} %get-tuple-element.19.w), custom_call_target="tpu_custom_call" | custom-call | tf_op jit(solution)/shard_map/keep_half/pallas_call | solution.py:234
  50.7 4.3 %collective-permute-done.came = bf16[256,1024]{1,0:T(8,128)(2,1)S(1)} collective-permute-done((bf16[256,1024]{1,0:T(8,128)(2,1)S(1)}, bf16[256,1024]{1,0:T(8,128)(2,1)S(1)}, u32[]{:S(2)}, u32[]{:S(2)}) %collective-permute-start) | collective-permute-done | bytes 524320 | tf_op jit(solution)/shard_map/ppermute | solution.py:413
  55.0 0.2 activate.1.mine
  55.2 1.3 collective-permute-start.1
  56.5 5.4 %collective-permute-done.1.other = bf16[256,512]{1,0:T(8,128)(2,1)S(1)} collective-permute-done((bf16[256,512]{1,0:T(8,128)(2,1)S(1)}, bf16[256,512]{1,0:T(8,128)(2,1)S(1)}, u32[]{:S(2)}, u32[]{:S(2)}) %collective-permute-start.1) | collective-permute-done | bytes 262176 | tf_op jit(solution)/shard_map/ppermute | solution.py:413
  61.8 0.0 slice-done
  61.8 0.0 slice-done.1
  61.8 4.1 %answers.1 = bf16[512,1536]{1,0:T(8,128)(2,1)} custom-call(s32[1]{0:T(128)} %bitcast.3.me, bf16[256,512]{1,0:T(8,128)(2,1)S(1)} %activate.1.mine, bf16[256,512]{1,0:T(8,128)(2,1)S(1)} %collective-permute-done.1.other, bf16[1024,3072]{1,0:T(8,128)(2,1)S(1)} %bitcast.12), custom_call_target="tpu_custom_call" | custom-call | tf_op jit(solution)/shard_map/answers/pallas_call | solution.py:281
  65.9 9.5 %all-to-all-start.1 = ((bf16[64,8,1536]{2,1,0:T(8,128)(2,1)}), bf16[64,8,1536]{2,1,0:T(8,128)(2,1)S(1)}, u32[]{:S(2)}, u32[]{:S(2)}) async-start(bf16[64,8,1536]{2,1,0:T(8,128)(2,1)} %bitcast.8), calls=%async_computation.1 | async-start | bytes 3145728 | tf_op jit(solution)/shard_map/all_to_all | solution.py:417
  75.5 0.0 collective-permute-done.2.refs_1_
  75.5 0.0 collective-permute-done.3.refs_2_
  75.5 4.0 %shared_in.2 = (bf16[384,512]{1,0:T(8,128)(2,1)S(1)}, f32[384,512]{1,0:T(8,128)}, bf16[64,3072]{1,0:T(8,128)(2,1)S(1)}, bf16[64,3072]{1,0:T(8,128)(2,1)S(1)}) custom-call(bf16[128,3072]{1,0:T(8,128)(2,1)S(1)} %copy-done.1, bf16[128,3072]{1,0:T(8,128)(2,1)S(1)} %collective-permute-done.2.refs_1_, bf16[128,3072]{1,0:T(8,128)(2,1)} %collective-permute-done.3.refs_2_, ...), custom_call_target="tpu_custom_call" | custom-call | tf_op jit(solution)/shard_map/shared_in/pallas_call | solution.py:318
  79.5 1.5 collective-permute-start.7
  81.0 1.8 %collective-permute-start.8 = (bf16[64,3072]{1,0:T(8,128)(2,1)S(1)}, bf16[64,3072]{1,0:T(8,128)(2,1)S(1)}, u32[]{:S(2)}, u32[]{:S(2)}) collective-permute-start(bf16[64,3072]{1,0:T(8,128)(2,1)S(1)} %get-tuple-element.29), channel_id=1, source_target_pairs={{0,96},{32,0},{64,32},{96,64},{1,97},{33,1},{65,33},{97,65},{2,98}... | collective-permute-start | bytes 1179656 | tf_op jit(solution)/shard_map/ppermute | solution.py:413
  82.7 1.2 collective-permute-start.4
  83.9 20.9 %collective-permute-done.7.refs_0_ = bf16[64,3072]{1,0:T(8,128)(2,1)S(1)} collective-permute-done((bf16[64,3072]{1,0:T(8,128)(2,1)S(1)}, bf16[64,3072]{1,0:T(8,128)(2,1)S(1)}, u32[]{:S(2)}, u32[]{:S(2)}) %collective-permute-start.7) | collective-permute-done | bytes 393248 | tf_op jit(solution)/shard_map/ppermute | solution.py:413
  104.8 0.0 collective-permute-done.8.refs_1_
  104.8 3.0 %shared_in.3 = (bf16[128,512]{1,0:T(8,128)(2,1)S(1)}, f32[128,512]{1,0:T(8,128)}) custom-call(bf16[64,3072]{1,0:T(8,128)(2,1)S(1)} %collective-permute-done.7.refs_0_, bf16[64,3072]{1,0:T(8,128)(2,1)S(1)} %collective-permute-done.8.refs_1_, bf16[2,3072,256]{2,1,0:T(8,128)(2,1)} %get-tuple-element.22.refs_3_.refs_2_), custom_call_target="tpu_custom_call" | custom-call | tf_op jit(solution)/shard_map/shared_in/pallas_call | solution.py:318
  107.8 1.2 collective-permute-start.9
  108.9 0.0 collective-permute-done.4.came
  109.0 0.0 copy-done
  109.0 0.0 copy-done.2
  109.0 0.6 shared_out.2
  109.6 0.0 copy-start.4
  109.6 0.7 copy-done.4
  110.3 0.0 collective-permute-start.5
  110.3 3.2 %collective-permute-start.6 = (bf16[128,3072]{1,0:T(8,128)(2,1)S(1)}, bf16[128,3072]{1,0:T(8,128)(2,1)S(1)}, u32[]{:S(2)}, u32[]{:S(2)}) collective-permute-start(bf16[128,3072]{1,0:T(8,128)(2,1)S(1)} %get-tuple-element.27), channel_id=1, source_target_pairs={{0,96},{32,0},{64,32},{96,64},{1,97},{33,1},{65,33},{97,65},{2,98}... | collective-permute-start | bytes 2359304 | tf_op jit(solution)/shard_map/ppermute | solution.py:413
  113.5 0.0 collective-permute-done.9.came
  113.5 0.7 shared_out.3
  114.2 0.4 collective-permute-start.10
  114.7 2.5 %combine_gates.1.gates = bf16[2,256,512]{2,1,0:T(8,128)(2,1)} custom-call(s32[8,128]{1,0:T(8,128)} %bitcast.18, s32[8,128]{1,0:T(8,128)} %bitcast.19, s32[1,64]{1,0:T(1,128)} %bitcast.21), custom_call_target="tpu_custom_call" | custom-call | tf_op jit(solution)/shard_map/combine_gates/pallas_call | solution.py:114
  117.1 2.6 %own_sum.1.base = f32[128,3072]{1,0:T(8,128)} custom-call(bf16[384,256]{1,0:T(8,128)(2,1)} %copy-done.4, bf16[256,3072]{1,0:T(8,128)(2,1)} %w.5), custom_call_target="tpu_custom_call" | custom-call | tf_op jit(solution)/shard_map/own_sum/pallas_call | solution.py:370
  119.7 27.9 %collective-permute-done.5.a = bf16[128,3072]{1,0:T(8,128)(2,1)S(1)} collective-permute-done((bf16[128,3072]{1,0:T(8,128)(2,1)S(1)}, bf16[128,3072]{1,0:T(8,128)(2,1)S(1)}, u32[]{:S(2)}, u32[]{:S(2)}) %collective-permute-start.5) | collective-permute-done | bytes 786464 | tf_op jit(solution)/shard_map/ppermute | solution.py:413
  147.6 0.0 collective-permute-done.6.b
  147.6 0.0 collective-permute-done.10.c
  147.6 0.0 all-to-all-done.1
  147.6 0.9 copy-done.5
  148.5 0.3 copy-done.6
  148.8 3.5 %mix.1 = bf16[128,3072]{1,0:T(8,128)(2,1)} custom-call(bf16[2,256,512]{2,1,0:T(8,128)(2,1)} %combine_gates.1.gates, bf16[512,1536]{1,0:T(8,128)(2,1)S(1)} %bitcast.13, f32[128,3072]{1,0:T(8,128)} %own_sum.1.base, bf16[128,3072]{1,0:T(8,128)(2,1)} %copy-done.5, bf16[128,3072]{1,0:T(8,128)(2,1)} %copy-done.6, bf16[128,3072]{1,0:T(8,128)(2,1)} %collective-permute-done.10.c), custom_call_target="tpu_custom_call" | custom-call | tf_op jit(solution)/shard_map/mix/pallas_call | solution.py:396
  (10 shorter events, 0.0 us)
Async XLA Ops:
  3.7 34.2 %all-to-all-start = ((bf16[64,8,1536]{2,1,0:T(8,128)(2,1)}), bf16[64,8,1536]{2,1,0:T(8,128)(2,1)S(1)}, u32[]{:S(2)}, u32[]{:S(2)}) async-start(bf16[64,8,1536]{2,1,0:T(8,128)(2,1)} %bitcast.16), calls=%async_computation | async-start | bytes 3145728 | tf_op jit(solution)/shard_map/all_to_all | solution.py:417
  37.9 5.4 %copy-start.1 = (bf16[128,3072]{1,0:T(8,128)(2,1)S(1)}, bf16[128,3072]{1,0:T(8,128)(2,1)}, u32[]{:S(2)}) copy-start(bf16[128,3072]{1,0:T(8,128)(2,1)} %refs_0_.1) | copy-start | bytes 2359300
  42.0 13.0 %collective-permute-start = (bf16[256,1024]{1,0:T(8,128)(2,1)S(1)}, bf16[256,1024]{1,0:T(8,128)(2,1)S(1)}, u32[]{:S(2)}, u32[]{:S(2)}) collective-permute-start(bf16[256,1024]{1,0:T(8,128)(2,1)S(1)} %get-tuple-element.21), channel_id=1, source_target_pairs={{0,1},{1,0},{2,3},{3,2},{4,5},{5,4},{6,7},{7,6},{8,9},{9,8},{10,11... | collective-permute-start | bytes 1572872 | tf_op jit(solution)/shard_map/ppermute | solution.py:413
  43.3 32.2 %collective-permute-start.2 = (bf16[128,3072]{1,0:T(8,128)(2,1)S(1)}, bf16[128,3072]{1,0:T(8,128)(2,1)S(1)}, u32[]{:S(2)}, u32[]{:S(2)}) collective-permute-start(bf16[128,3072]{1,0:T(8,128)(2,1)S(1)} %copy-done.1), channel_id=1, source_target_pairs={{0,32},{32,64},{64,96},{96,0},{1,33},{33,65},{65,97},{97,1},{2,34}... | collective-permute-start | bytes 2359304 | tf_op jit(solution)/shard_map/ppermute | solution.py:413
  43.3 32.2 %collective-permute-start.3 = (bf16[128,3072]{1,0:T(8,128)(2,1)S(1)}, bf16[128,3072]{1,0:T(8,128)(2,1)}, u32[]{:S(2)}, u32[]{:S(2)}) collective-permute-start(bf16[128,3072]{1,0:T(8,128)(2,1)S(1)} %copy-done.1), channel_id=1, source_target_pairs={{0,96},{32,0},{64,32},{96,64},{1,97},{33,1},{65,33},{97,65},{2,98}... | collective-permute-start | bytes 2359304 | tf_op jit(solution)/shard_map/ppermute | solution.py:413
  46.5 15.3 %slice-start = ((s8[6291456]{0:T(1024)(128)(4,1)}), s8[4194304]{0:T(1024)(128)(4,1)S(1)}, s32[]{:S(2)}) async-start(s8[6291456]{0:T(1024)(128)(4,1)} %bitcast.10), calls=%async_computation.2 | async-start | bytes 8388608
  46.5 15.3 %slice-start.1 = ((s8[6291456]{0:T(1024)(128)(4,1)}), s8[2097152]{0:T(1024)(128)(4,1)S(1)}, s32[]{:S(2)}) async-start(s8[6291456]{0:T(1024)(128)(4,1)} %bitcast.10), calls=%async_computation.3 | async-start | bytes 4194304
  55.2 6.7 %collective-permute-start.1 = (bf16[256,512]{1,0:T(8,128)(2,1)S(1)}, bf16[256,512]{1,0:T(8,128)(2,1)S(1)}, u32[]{:S(2)}, u32[]{:S(2)}) collective-permute-start(bf16[256,512]{1,0:T(8,128)(2,1)S(1)} %activate.1.mine), channel_id=1, source_target_pairs={{0,1},{1,0},{2,3},{3,2},{4,5},{5,4},{6,7},{7,6},{8,9},{9,8},{10,11... | collective-permute-start | bytes 786440 | tf_op jit(solution)/shard_map/ppermute | solution.py:413
  65.9 81.7 %all-to-all-start.1 = ((bf16[64,8,1536]{2,1,0:T(8,128)(2,1)}), bf16[64,8,1536]{2,1,0:T(8,128)(2,1)S(1)}, u32[]{:S(2)}, u32[]{:S(2)}) async-start(bf16[64,8,1536]{2,1,0:T(8,128)(2,1)} %bitcast.8), calls=%async_computation.1 | async-start | bytes 3145728 | tf_op jit(solution)/shard_map/all_to_all | solution.py:417
  79.5 25.3 %collective-permute-start.7 = (bf16[64,3072]{1,0:T(8,128)(2,1)S(1)}, bf16[64,3072]{1,0:T(8,128)(2,1)S(1)}, u32[]{:S(2)}, u32[]{:S(2)}) collective-permute-start(bf16[64,3072]{1,0:T(8,128)(2,1)S(1)} %get-tuple-element.28), channel_id=1, source_target_pairs={{0,32},{32,64},{64,96},{96,0},{1,33},{33,65},{65,97},{97,1},{2,34}... | collective-permute-start | bytes 1179656 | tf_op jit(solution)/shard_map/ppermute | solution.py:413
  81.0 23.8 %collective-permute-start.8 = (bf16[64,3072]{1,0:T(8,128)(2,1)S(1)}, bf16[64,3072]{1,0:T(8,128)(2,1)S(1)}, u32[]{:S(2)}, u32[]{:S(2)}) collective-permute-start(bf16[64,3072]{1,0:T(8,128)(2,1)S(1)} %get-tuple-element.29), channel_id=1, source_target_pairs={{0,96},{32,0},{64,32},{96,64},{1,97},{33,1},{65,33},{97,65},{2,98}... | collective-permute-start | bytes 1179656 | tf_op jit(solution)/shard_map/ppermute | solution.py:413
  82.7 26.2 %copy-start = (bf16[256,3072]{1,0:T(8,128)(2,1)S(1)}, bf16[256,3072]{1,0:T(8,128)(2,1)}, u32[]{:S(2)}) copy-start(bf16[256,3072]{1,0:T(8,128)(2,1)} %w.5) | copy-start | bytes 4718596
  82.7 26.2 %copy-start.2 = (f32[384,512]{1,0:T(8,128)S(1)}, f32[384,512]{1,0:T(8,128)}, u32[]{:S(2)}) copy-start(f32[384,512]{1,0:T(8,128)} %get-tuple-element.23.kept) | copy-start | bytes 2359300
  82.7 26.2 %collective-permute-start.4 = (bf16[384,512]{1,0:T(8,128)(2,1)S(1)}, bf16[384,512]{1,0:T(8,128)(2,1)S(1)}, u32[]{:S(2)}, u32[]{:S(2)}) collective-permute-start(bf16[384,512]{1,0:T(8,128)(2,1)S(1)} %get-tuple-element.24), channel_id=1, source_target_pairs={{0,1},{1,0},{2,3},{3,2},{4,5},{5,4},{6,7},{7,6},{8,9},{9,8},{10,11... | collective-permute-start | bytes 1179656 | tf_op jit(solution)/shard_map/ppermute | solution.py:413
  107.8 5.8 %copy-start.3 = (f32[128,512]{1,0:T(8,128)S(1)}, f32[128,512]{1,0:T(8,128)}, u32[]{:S(2)}) copy-start(f32[128,512]{1,0:T(8,128)} %get-tuple-element.30.kept) | copy-start | bytes 786436
  107.8 5.8 %collective-permute-start.9 = (bf16[128,512]{1,0:T(8,128)(2,1)S(1)}, bf16[128,512]{1,0:T(8,128)(2,1)S(1)}, u32[]{:S(2)}, u32[]{:S(2)}) collective-permute-start(bf16[128,512]{1,0:T(8,128)(2,1)S(1)} %get-tuple-element.31), channel_id=1, source_target_pairs={{0,1},{1,0},{2,3},{3,2},{4,5},{5,4},{6,7},{7,6},{8,9},{9,8},{10,11... | collective-permute-start | bytes 393224 | tf_op jit(solution)/shard_map/ppermute | solution.py:413
  109.6 0.7 copy-start.4
  110.3 37.3 %collective-permute-start.5 = (bf16[128,3072]{1,0:T(8,128)(2,1)S(1)}, bf16[128,3072]{1,0:T(8,128)(2,1)S(1)}, u32[]{:S(2)}, u32[]{:S(2)}) collective-permute-start(bf16[128,3072]{1,0:T(8,128)(2,1)S(1)} %get-tuple-element.26), channel_id=1, source_target_pairs={{0,32},{32,64},{64,96},{96,0},{1,33},{33,65},{65,97},{97,1},{2,34}... | collective-permute-start | bytes 2359304 | tf_op jit(solution)/shard_map/ppermute | solution.py:413
  110.3 37.3 %collective-permute-start.6 = (bf16[128,3072]{1,0:T(8,128)(2,1)S(1)}, bf16[128,3072]{1,0:T(8,128)(2,1)S(1)}, u32[]{:S(2)}, u32[]{:S(2)}) collective-permute-start(bf16[128,3072]{1,0:T(8,128)(2,1)S(1)} %get-tuple-element.27), channel_id=1, source_target_pairs={{0,96},{32,0},{64,32},{96,64},{1,97},{33,1},{65,33},{97,65},{2,98}... | collective-permute-start | bytes 2359304 | tf_op jit(solution)/shard_map/ppermute | solution.py:413
  114.2 33.4 %collective-permute-start.10 = (bf16[128,3072]{1,0:T(8,128)(2,1)S(1)}, bf16[128,3072]{1,0:T(8,128)(2,1)}, u32[]{:S(2)}, u32[]{:S(2)}) collective-permute-start(bf16[128,3072]{1,0:T(8,128)(2,1)S(1)} %get-tuple-element.32), channel_id=1, source_target_pairs={{0,64},{32,96},{64,0},{96,32},{1,65},{33,97},{65,1},{97,33},{2,66}... | collective-permute-start | bytes 2359304 | tf_op jit(solution)/shard_map/ppermute | solution.py:413
  147.6 0.9 copy-start.5
  147.6 1.2 copy-start.6

commit v2 on v1

--- a/solution.py
+++ b/solution.py
@@ -287,36 +287,40 @@
     )(me, mine, other, w)
 
 
-def shared_kernel(*refs, count, ahead):
-    pieces, w, sent, kept = refs[:count], *refs[count : count + 3]
+def shared_kernel(*refs, count, cuts, ahead):
+    pieces, w = refs[:count], refs[count]
+    kept, *sent = refs[count + 1 : count + 2 + len(cuts)]
     pre = dot(jnp.concatenate([piece[...] for piece in pieces], axis=0), w[0])
-    sent[...] = pre.astype(BF)
     kept[...] = pre
+    start = 0
+    for rows, out in zip(cuts, sent):
+        out[...] = pre[start : start + rows].astype(BF)
+        start += rows
     if ahead:
 
         @pl.when(pl.program_id(0) == 0)
         def _():
-            up, down = refs[count + 3 :]
+            up, down = refs[-2:]
             rows = up.shape[0]
-            up[...] = pieces[1][:rows, :]
-            down[...] = pieces[2][rows:, :]
-
-
-def shared_in_part(pieces, w, ahead):
+            up[...] = pieces[0][:rows, :]
+            down[...] = pieces[1][rows:, :]
+
+
+def shared_in_part(pieces, w, cuts, ahead=0):
     rows = sum(piece.shape[0] for piece in pieces)
     blocks, width, block = w.shape
-    part = pl.BlockSpec((rows, block), lambda j: (0, j))
-    out_specs = [part, part]
-    out_shape = [
-        jax.ShapeDtypeStruct((rows, blocks * block), BF),
-        pltpu.HBM((rows, blocks * block), F32),
-    ]
+
+    def part(rows):
+        return pl.BlockSpec((rows, block), lambda j: (0, j))
+
+    out_specs = [part(rows)] + [part(cut) for cut in cuts]
+    out_shape = [pltpu.HBM((rows, blocks * block), F32)]
+    out_shape += [jax.ShapeDtypeStruct((cut, blocks * block), BF) for cut in cuts]
     if ahead:
-        shape = (pieces[0].shape[0] // 2, width)
-        out_specs += [pl.BlockSpec(shape, lambda j: (0, 0))] * 2
-        out_shape += [jax.ShapeDtypeStruct(shape, BF)] * 2
-    return pl.pallas_call(
-        functools.partial(shared_kernel, count=len(pieces), ahead=ahead),
+        out_specs += [pl.BlockSpec((ahead, width), lambda j: (0, 0))] * 2
+        out_shape += [jax.ShapeDtypeStruct((ahead, width), BF)] * 2
+    return pl.pallas_call(
+        functools.partial(shared_kernel, count=len(pieces), cuts=cuts, ahead=ahead),
         grid=(blocks,),
         in_specs=[pl.BlockSpec(memory_space=pltpu.VMEM)] * len(pieces)
         + [pl.BlockSpec((1, width, block), lambda j: (j, 0, 0))],
@@ -339,46 +343,44 @@
     )
 
 
-def out_kernel(kept, came, w, act_out, *outs):
-    act = paired_act(kept[...], came[...])
-    act_out[...] = act
+def out_kernel(kept, came, w, *outs):
     rows = outs[0].shape[0]
-    first = act.shape[0] - rows * len(outs)
-    total = dot(act[first:, :], w[...])
+    total = dot(paired_act(kept[: came.shape[0], :], came[...]), w[...])
     for i, out in enumerate(outs):
         out[...] = total[i * rows : (i + 1) * rows].astype(BF)
 
 
-def shared_out_part(kept, came, w, count, rows):
-    units, width = w.shape
+def shared_out_part(kept, came, w, count):
+    rows, width = came.shape[0] // count, w.shape[1]
     return pl.pallas_call(
         out_kernel,
         in_specs=[pl.BlockSpec(memory_space=pltpu.VMEM)] * 3,
-        out_shape=(jax.ShapeDtypeStruct((kept.shape[0], units), BF),)
-        + (jax.ShapeDtypeStruct((rows, width), BF),) * count,
+        out_shape=(jax.ShapeDtypeStruct((rows, width), BF),) * count,
         compiler_params=params(),
         name="shared_out",
     )(kept, came, w)
 
 
-def base_kernel(act, w, out):
-    out[...] = dot(act[...], w[...])
-
-
-def own_sum(act, w, tokens, block=1536):
+def base_kernel(kept, came, w, out):
+    out[...] = dot(paired_act(kept[...], came[...]), w[...])
+
+
+def own_sum(kept, came, w, block=1536):
     units, width = w.shape
+    tokens = came.shape[0]
     return pl.pallas_call(
         base_kernel,
         grid=(width // block,),
         in_specs=[
-            pl.BlockSpec((tokens, units), lambda j: (0, 0)),
+            pl.BlockSpec((tokens, kept.shape[1]), lambda j: (1, 0)),
+            pl.BlockSpec(came.shape, lambda j: (0, 0)),
             pl.BlockSpec((units, block), lambda j: (0, j)),
         ],
         out_specs=pl.BlockSpec((tokens, block), lambda j: (0, j)),
         out_shape=pltpu.HBM((tokens, width), F32),
         compiler_params=params(),
         name="own_sum",
-    )(far(act), far(w))
+    )(far(kept), far(came), far(w))
 
 
 def mix_kernel(gates, back, base, a, b, c, out):
@@ -431,7 +433,9 @@
     arrived = exchange(send_rows.reshape(slots, 2 * CAP, half))
     arrived = arrived.reshape(-1, half)
     w_in, w_shared = split_gate_up(expert_in[0], shared_in)
-    n_sent, n_kept, ahead, behind = shared_in_part((hidden, prev, nxt), w_shared, True)
+    n_kept, n_sent, ahead, behind = shared_in_part(
+        (prev, nxt), w_shared, (2 * tokens,), tokens // 2
+    )
     n_came = shift(n_sent, "tensor", 1)
     far_a = shift(ahead, "dp", 1)
     far_b = shift(behind, "dp", -1)
@@ -439,22 +443,25 @@
     x, sent = send_half(arrived, w_in, me)
     came = shift(sent, "tensor", 1)
     kept = keep_half(x, w_in, me)
-    own_act, down, up = shared_out_part(n_kept, n_came, shared_out, 2, tokens)
+    down, up = shared_out_part(n_kept, n_came, shared_out, 2)
     from_prev = shift(up, "dp", 1)
     from_next = shift(down, "dp", -1)
-    f_sent, f_kept = shared_in_part((far_a, far_b), w_shared, False)
+    f_kept, f_sent, own_sent = shared_in_part(
+        (far_a, far_b, hidden), w_shared, (tokens, tokens)
+    )
     f_came = shift(f_sent, "tensor", 1)
+    own_came = shift(own_sent, "tensor", 1)
 
     act = activate(kept, came)
     act_other = shift(act, "tensor", 1)
-    _, far_part = shared_out_part(f_kept, f_came, shared_out, 1, tokens)
+    (far_part,) = shared_out_part(f_kept, f_came, shared_out, 1)
     from_far = shift(far_part, "dp", 2)
 
     rows = answers(act, act_other, expert_out[0], me)
     back = exchange(rows.reshape(slots, 2 * CAP, half))
     back = back.reshape(-1, half)
     gates = combine_gates(expert_ids, gate_fixed, slot_expert)
-    base = own_sum(own_act, shared_out, tokens)
+    base = own_sum(f_kept, own_came, shared_out)
     return mix(gates, back, base, (from_prev, from_next, from_far))
 
 

time: 153 us -> 152 us (level)
  starting transfers between devices: 36 us -> 37.6 us
  waiting for transfers between devices: 68.3 us -> 66.7 us
    ppermute x11 -> x12, starting transfers between devices: 15.1 us -> 16.6 us  [shift(): lax.ppermute(array, axis, [(i, (i + by) % size) for i in range(size)])]
    ppermute x11 -> x12, waiting for transfers between devices: 58.5 us -> 56.9 us  [shift(): lax.ppermute(array, axis, [(i, (i + by) % size) for i in range(size)])]
  transfers between devices with their start and end apart: 13 -> 14, of which waited for: 5 -> 7; matrix products, arithmetic and copies ran while one was open for 0% -> 0% of each run, Pallas kernels for 23% -> 23%
where the time goes in v2:
time: 152 us
  waiting for transfers between devices  66.7 us (44%)
  Pallas kernels  45.7 us (30%)
  starting transfers between devices  37.6 us (25%)
  local copies, waits for them, and re-layouts  1.84 us (1%)
    ppermute x12, waiting for transfers between devices, shift(): lax.ppermute(array, axis, [(i, (i + by) % size) for i in range(size)])  56.9 us
    all_to_all x2, starting transfers between devices, exchange(): lax.all_to_all(rows, ('dp', 'expert'), split_axis=0, concat_axis=0, tiled...  21 us
    ppermute x12, starting transfers between devices, shift(): lax.ppermute(array, axis, [(i, (i + by) % size) for i in range(size)])  16.6 us
    pallas_call x1, Pallas kernels, split_gate_up(): pl.pallas_call(functools.partial(split_kernel, sub=sub), grid=(width // d...  12.9 us
    all_to_all x2, waiting for transfers between devices, exchange(): lax.all_to_all(rows, ('dp', 'expert'), split_axis=0, concat_axis=0, tiled...  9.76 us
    pallas_call x2, Pallas kernels, shared_in_part(): pl.pallas_call(functools.partial(shared_kernel, count=len(pieces), cuts=c...  6.88 us
    pallas_call x1, Pallas kernels, keep_half(): pl.pallas_call(keep_kernel, in_specs=[pl.BlockSpec(memory_space=pltpu.SME...  4.17 us
    pallas_call x1, Pallas kernels, send_half(): pl.pallas_call(send_kernel, in_specs=[pl.BlockSpec(memory_space=pltpu.SME...  4.11 us
  transfers between devices with their start and end apart: 14, of which 7 were waited for; matrix products, arithmetic and copies ran while one was open for 0% of the time, Pallas kernels for 23%

profile of v2, /device:TPU:4, one launch (start us, length us, event | category | flops | bytes accessed | tf_op | source)
XLA Modules:
  0.0 152.0 jit_solution(6922409914588149526)
XLA Ops:
  0.0 3.7 %route.1 = bf16[512,1536]{1,0:T(8,128)(2,1)} custom-call(s32[8,128]{1,0:T(8,128)} %bitcast.17, s32[1,64]{1,0:T(1,128)} %bitcast.20, bf16[128,3072]{1,0:T(8,128)(2,1)} %refs_2_.1, bf16[128,3072]{1,0:T(8,128)(2,1)} %refs_2_.1), custom_call_target="tpu_custom_call" | custom-call | tf_op jit(solution)/shard_map/route/pallas_call | solution.py:78
  3.7 11.5 %all-to-all-start = ((bf16[64,8,1536]{2,1,0:T(8,128)(2,1)}), bf16[64,8,1536]{2,1,0:T(8,128)(2,1)S(1)}, u32[]{:S(2)}, u32[]{:S(2)}) async-start(bf16[64,8,1536]{2,1,0:T(8,128)(2,1)} %bitcast.16), calls=%async_computation | async-start | bytes 3145728 | tf_op jit(solution)/shard_map/all_to_all | solution.py:419
  15.2 12.9 %split.1 = (bf16[4,3072,512]{2,1,0:T(8,128)(2,1)}, bf16[2,3072,256]{2,1,0:T(8,128)(2,1)}) custom-call(bf16[3072,2,1024]{2,1,0:T(2,128)(2,1)} %bitcast.15, bf16[3072,2,256]{2,1,0:T(2,128)(2,1)} %w_shared.1), custom_call_target="tpu_custom_call" | custom-call | tf_op jit(solution)/shard_map/split/pallas_call | solution.py:154
  28.1 9.8 %all-to-all-done = bf16[64,8,1536]{2,1,0:T(8,128)(2,1)S(1)} async-done(((bf16[64,8,1536]{2,1,0:T(8,128)(2,1)}), bf16[64,8,1536]{2,1,0:T(8,128)(2,1)S(1)}, u32[]{:S(2)}, u32[]{:S(2)}) %all-to-all-start) | async-done | bytes 1572896 | tf_op jit(solution)/shard_map/all_to_all | solution.py:419
  37.9 4.1 %send_half.1 = (bf16[256,3072]{1,0:T(8,128)(2,1)S(1)}, bf16[256,1024]{1,0:T(8,128)(2,1)S(1)}) custom-call(s32[1]{0:T(128)} %bitcast.3.me, bf16[512,1536]{1,0:T(8,128)(2,1)S(1)} %bitcast.14, bf16[4,3072,512]{2,1,0:T(8,128)(2,1)} %get-tuple-element.18.w), custom_call_target="tpu_custom_call" | custom-call | tf_op jit(solution)/shard_map/send_half/pallas_call | solution.py:215
  42.0 1.3 collective-permute-start
  43.3 0.0 copy-done.1
  43.3 0.0 collective-permute-start.2
  43.3 3.2 %collective-permute-start.3 = (bf16[128,3072]{1,0:T(8,128)(2,1)S(1)}, bf16[128,3072]{1,0:T(8,128)(2,1)}, u32[]{:S(2)}, u32[]{:S(2)}) collective-permute-start(bf16[128,3072]{1,0:T(8,128)(2,1)S(1)} %copy-done.1), channel_id=1, source_target_pairs={{0,96},{32,0},{64,32},{96,64},{1,97},{33,1},{65,33},{97,65},{2,98}... | collective-permute-start | bytes 2359304 | tf_op jit(solution)/shard_map/ppermute | solution.py:415
  46.5 4.2 %keep_half.1.kept = f32[256,1024]{1,0:T(8,128)S(1)} custom-call(s32[1]{0:T(128)} %bitcast.3.me, bf16[256,3072]{1,0:T(8,128)(2,1)S(1)} %get-tuple-element.19.x, bf16[4,3072,512]{2,1,0:T(8,128)(2,1)} %get-tuple-element.18.w), custom_call_target="tpu_custom_call" | custom-call | tf_op jit(solution)/shard_map/keep_half/pallas_call | solution.py:234
  50.7 4.3 %collective-permute-done.came = bf16[256,1024]{1,0:T(8,128)(2,1)S(1)} collective-permute-done((bf16[256,1024]{1,0:T(8,128)(2,1)S(1)}, bf16[256,1024]{1,0:T(8,128)(2,1)S(1)}, u32[]{:S(2)}, u32[]{:S(2)}) %collective-permute-start) | collective-permute-done | bytes 524320 | tf_op jit(solution)/shard_map/ppermute | solution.py:415
  55.0 0.2 activate.1.mine
  55.2 1.3 collective-permute-start.1
  56.5 5.4 %collective-permute-done.1.other = bf16[256,512]{1,0:T(8,128)(2,1)S(1)} collective-permute-done((bf16[256,512]{1,0:T(8,128)(2,1)S(1)}, bf16[256,512]{1,0:T(8,128)(2,1)S(1)}, u32[]{:S(2)}, u32[]{:S(2)}) %collective-permute-start.1) | collective-permute-done | bytes 262176 | tf_op jit(solution)/shard_map/ppermute | solution.py:415
  61.8 0.0 slice-done
  61.8 0.0 slice-done.1
  61.8 4.1 %answers.1 = bf16[512,1536]{1,0:T(8,128)(2,1)} custom-call(s32[1]{0:T(128)} %bitcast.3.me, bf16[256,512]{1,0:T(8,128)(2,1)S(1)} %activate.1.mine, bf16[256,512]{1,0:T(8,128)(2,1)S(1)} %collective-permute-done.1.other, bf16[1024,3072]{1,0:T(8,128)(2,1)S(1)} %bitcast.12), custom_call_target="tpu_custom_call" | custom-call | tf_op jit(solution)/shard_map/answers/pallas_call | solution.py:281
  65.9 9.5 %all-to-all-start.1 = ((bf16[64,8,1536]{2,1,0:T(8,128)(2,1)}), bf16[64,8,1536]{2,1,0:T(8,128)(2,1)S(1)}, u32[]{:S(2)}, u32[]{:S(2)}) async-start(bf16[64,8,1536]{2,1,0:T(8,128)(2,1)} %bitcast.8), calls=%async_computation.1 | async-start | bytes 3145728 | tf_op jit(solution)/shard_map/all_to_all | solution.py:419
  75.5 0.0 collective-permute-done.2.refs_0_
  75.5 0.0 collective-permute-done.3.refs_1_
  75.5 3.5 %shared_in.2 = (f32[256,512]{1,0:T(8,128)}, bf16[256,512]{1,0:T(8,128)(2,1)S(1)}, bf16[64,3072]{1,0:T(8,128)(2,1)S(1)}, bf16[64,3072]{1,0:T(8,128)(2,1)S(1)}) custom-call(bf16[128,3072]{1,0:T(8,128)(2,1)S(1)} %collective-permute-done.2.refs_0_, bf16[128,3072]{1,0:T(8,128)(2,1)} %collective-permute-done.3.refs_1_, ...), custom_call_target="tpu_custom_call" | custom-call | tf_op jit(solution)/shard_map/shared_in/pallas_call | solution.py:322
  79.0 1.5 collective-permute-start.4
  80.5 1.8 %collective-permute-start.5 = (bf16[64,3072]{1,0:T(8,128)(2,1)S(1)}, bf16[64,3072]{1,0:T(8,128)(2,1)S(1)}, u32[]{:S(2)}, u32[]{:S(2)}) collective-permute-start(bf16[64,3072]{1,0:T(8,128)(2,1)S(1)} %get-tuple-element.23), channel_id=1, source_target_pairs={{0,96},{32,0},{64,32},{96,64},{1,97},{33,1},{65,33},{97,65},{2,98}... | collective-permute-start | bytes 1179656 | tf_op jit(solution)/shard_map/ppermute | solution.py:415
  82.3 1.2 collective-permute-start.7
  83.5 21.3 %collective-permute-done.4.refs_0_ = bf16[64,3072]{1,0:T(8,128)(2,1)S(1)} collective-permute-done((bf16[64,3072]{1,0:T(8,128)(2,1)S(1)}, bf16[64,3072]{1,0:T(8,128)(2,1)S(1)}, u32[]{:S(2)}, u32[]{:S(2)}) %collective-permute-start.4) | collective-permute-done | bytes 393248 | tf_op jit(solution)/shard_map/ppermute | solution.py:415
  104.7 0.0 collective-permute-done.5.refs_1_
  104.7 3.3 %shared_in.3 = (f32[256,512]{1,0:T(8,128)}, bf16[128,512]{1,0:T(8,128)(2,1)S(1)}, bf16[128,512]{1,0:T(8,128)(2,1)S(1)}) custom-call(bf16[64,3072]{1,0:T(8,128)(2,1)S(1)} %collective-permute-done.4.refs_0_, bf16[64,3072]{1,0:T(8,128)(2,1)S(1)} %collective-permute-done.5.refs_1_, bf16[128,3072]{1,0:T(8,128)(2,1)S(1)} %copy-done.1, ...), custom_call_target="tpu_custom_call" | custom-call | tf_op jit(solution)/shard_map/shared_in/pallas_call | solution.py:322
  108.1 1.2 collective-permute-start.10
  109.3 0.0 collective-permute-done.7.came
  109.3 0.0 copy-done.3
  109.3 0.6 shared_out.2
  109.9 0.1 collective-permute-start.8
  110.0 3.2 %collective-permute-start.9 = (bf16[128,3072]{1,0:T(8,128)(2,1)S(1)}, bf16[128,3072]{1,0:T(8,128)(2,1)S(1)}, u32[]{:S(2)}, u32[]{:S(2)}) collective-permute-start(bf16[128,3072]{1,0:T(8,128)(2,1)S(1)} %get-tuple-element.29), channel_id=1, source_target_pairs={{0,96},{32,0},{64,32},{96,64},{1,97},{33,1},{65,33},{97,65},{2,98}... | collective-permute-start | bytes 2359304 | tf_op jit(solution)/shard_map/ppermute | solution.py:415
  113.2 0.3 collective-permute-done.10.came
  113.5 0.4 shared_out.3
  113.9 0.7 collective-permute-start.11
  114.7 1.2 collective-permute-start.6
  115.9 2.5 %combine_gates.1.gates = bf16[2,256,512]{2,1,0:T(8,128)(2,1)} custom-call(s32[8,128]{1,0:T(8,128)} %bitcast.18, s32[8,128]{1,0:T(8,128)} %bitcast.19, s32[1,64]{1,0:T(1,128)} %bitcast.21), custom_call_target="tpu_custom_call" | custom-call | tf_op jit(solution)/shard_map/combine_gates/pallas_call | solution.py:114
  118.4 1.3 collective-permute-done.6.came
  119.7 0.7 copy-done.6
  120.3 2.7 %own_sum.1.base = f32[128,3072]{1,0:T(8,128)} custom-call(f32[256,512]{1,0:T(8,128)} %get-tuple-element.24.kept, bf16[128,512]{1,0:T(8,128)(2,1)} %copy-done.6, bf16[256,3072]{1,0:T(8,128)(2,1)} %w.5), custom_call_target="tpu_custom_call" | custom-call | tf_op jit(solution)/shard_map/own_sum/pallas_call | solution.py:371
  123.0 24.2 %collective-permute-done.8.a = bf16[128,3072]{1,0:T(8,128)(2,1)S(1)} collective-permute-done((bf16[128,3072]{1,0:T(8,128)(2,1)S(1)}, bf16[128,3072]{1,0:T(8,128)(2,1)S(1)}, u32[]{:S(2)}, u32[]{:S(2)}) %collective-permute-start.8) | collective-permute-done | bytes 786464 | tf_op jit(solution)/shard_map/ppermute | solution.py:415
  147.2 0.0 collective-permute-done.9.b
  147.3 0.0 collective-permute-done.11.c
  147.3 0.0 all-to-all-done.1
  147.3 0.9 copy-done.4
  148.1 0.3 copy-done.5
  148.4 3.5 %mix.1 = bf16[128,3072]{1,0:T(8,128)(2,1)} custom-call(bf16[2,256,512]{2,1,0:T(8,128)(2,1)} %combine_gates.1.gates, bf16[512,1536]{1,0:T(8,128)(2,1)S(1)} %bitcast.13, f32[128,3072]{1,0:T(8,128)} %own_sum.1.base, bf16[128,3072]{1,0:T(8,128)(2,1)} %copy-done.4, bf16[128,3072]{1,0:T(8,128)(2,1)} %copy-done.5, bf16[128,3072]{1,0:T(8,128)(2,1)} %collective-permute-done.11.c), custom_call_target="tpu_custom_call" | custom-call | tf_op jit(solution)/shard_map/mix/pallas_call | solution.py:398
  (12 shorter events, 0.0 us)
Async XLA Ops:
  3.7 34.2 %all-to-all-start = ((bf16[64,8,1536]{2,1,0:T(8,128)(2,1)}), bf16[64,8,1536]{2,1,0:T(8,128)(2,1)S(1)}, u32[]{:S(2)}, u32[]{:S(2)}) async-start(bf16[64,8,1536]{2,1,0:T(8,128)(2,1)} %bitcast.16), calls=%async_computation | async-start | bytes 3145728 | tf_op jit(solution)/shard_map/all_to_all | solution.py:419
  37.9 5.4 %copy-start.1 = (bf16[128,3072]{1,0:T(8,128)(2,1)S(1)}, bf16[128,3072]{1,0:T(8,128)(2,1)}, u32[]{:S(2)}) copy-start(bf16[128,3072]{1,0:T(8,128)(2,1)} %refs_2_.1) | copy-start | bytes 2359300
  42.0 13.0 %collective-permute-start = (bf16[256,1024]{1,0:T(8,128)(2,1)S(1)}, bf16[256,1024]{1,0:T(8,128)(2,1)S(1)}, u32[]{:S(2)}, u32[]{:S(2)}) collective-permute-start(bf16[256,1024]{1,0:T(8,128)(2,1)S(1)} %get-tuple-element.20), channel_id=1, source_target_pairs={{0,1},{1,0},{2,3},{3,2},{4,5},{5,4},{6,7},{7,6},{8,9},{9,8},{10,11... | collective-permute-start | bytes 1572872 | tf_op jit(solution)/shard_map/ppermute | solution.py:415
  43.3 32.2 %collective-permute-start.2 = (bf16[128,3072]{1,0:T(8,128)(2,1)S(1)}, bf16[128,3072]{1,0:T(8,128)(2,1)S(1)}, u32[]{:S(2)}, u32[]{:S(2)}) collective-permute-start(bf16[128,3072]{1,0:T(8,128)(2,1)S(1)} %copy-done.1), channel_id=1, source_target_pairs={{0,32},{32,64},{64,96},{96,0},{1,33},{33,65},{65,97},{97,1},{2,34}... | collective-permute-start | bytes 2359304 | tf_op jit(solution)/shard_map/ppermute | solution.py:415
  43.3 32.2 %collective-permute-start.3 = (bf16[128,3072]{1,0:T(8,128)(2,1)S(1)}, bf16[128,3072]{1,0:T(8,128)(2,1)}, u32[]{:S(2)}, u32[]{:S(2)}) collective-permute-start(bf16[128,3072]{1,0:T(8,128)(2,1)S(1)} %copy-done.1), channel_id=1, source_target_pairs={{0,96},{32,0},{64,32},{96,64},{1,97},{33,1},{65,33},{97,65},{2,98}... | collective-permute-start | bytes 2359304 | tf_op jit(solution)/shard_map/ppermute | solution.py:415
  46.5 15.3 %slice-start = ((s8[6291456]{0:T(1024)(128)(4,1)}), s8[4194304]{0:T(1024)(128)(4,1)S(1)}, s32[]{:S(2)}) async-start(s8[6291456]{0:T(1024)(128)(4,1)} %bitcast.10), calls=%async_computation.2 | async-start | bytes 8388608
  46.5 15.3 %slice-start.1 = ((s8[6291456]{0:T(1024)(128)(4,1)}), s8[2097152]{0:T(1024)(128)(4,1)S(1)}, s32[]{:S(2)}) async-start(s8[6291456]{0:T(1024)(128)(4,1)} %bitcast.10), calls=%async_computation.3 | async-start | bytes 4194304
  55.2 6.7 %collective-permute-start.1 = (bf16[256,512]{1,0:T(8,128)(2,1)S(1)}, bf16[256,512]{1,0:T(8,128)(2,1)S(1)}, u32[]{:S(2)}, u32[]{:S(2)}) collective-permute-start(bf16[256,512]{1,0:T(8,128)(2,1)S(1)} %activate.1.mine), channel_id=1, source_target_pairs={{0,1},{1,0},{2,3},{3,2},{4,5},{5,4},{6,7},{7,6},{8,9},{9,8},{10,11... | collective-permute-start | bytes 786440 | tf_op jit(solution)/shard_map/ppermute | solution.py:415
  65.9 81.3 %all-to-all-start.1 = ((bf16[64,8,1536]{2,1,0:T(8,128)(2,1)}), bf16[64,8,1536]{2,1,0:T(8,128)(2,1)S(1)}, u32[]{:S(2)}, u32[]{:S(2)}) async-start(bf16[64,8,1536]{2,1,0:T(8,128)(2,1)} %bitcast.8), calls=%async_computation.1 | async-start | bytes 3145728 | tf_op jit(solution)/shard_map/all_to_all | solution.py:419
  79.0 25.7 %collective-permute-start.4 = (bf16[64,3072]{1,0:T(8,128)(2,1)S(1)}, bf16[64,3072]{1,0:T(8,128)(2,1)S(1)}, u32[]{:S(2)}, u32[]{:S(2)}) collective-permute-start(bf16[64,3072]{1,0:T(8,128)(2,1)S(1)} %get-tuple-element.22), channel_id=1, source_target_pairs={{0,32},{32,64},{64,96},{96,0},{1,33},{33,65},{65,97},{97,1},{2,34}... | collective-permute-start | bytes 1179656 | tf_op jit(solution)/shard_map/ppermute | solution.py:415
  80.5 24.2 %collective-permute-start.5 = (bf16[64,3072]{1,0:T(8,128)(2,1)S(1)}, bf16[64,3072]{1,0:T(8,128)(2,1)S(1)}, u32[]{:S(2)}, u32[]{:S(2)}) collective-permute-start(bf16[64,3072]{1,0:T(8,128)(2,1)S(1)} %get-tuple-element.23), channel_id=1, source_target_pairs={{0,96},{32,0},{64,32},{96,64},{1,97},{33,1},{65,33},{97,65},{2,98}... | collective-permute-start | bytes 1179656 | tf_op jit(solution)/shard_map/ppermute | solution.py:415
  82.3 27.0 %copy-start = (bf16[256,3072]{1,0:T(8,128)(2,1)S(1)}, bf16[256,3072]{1,0:T(8,128)(2,1)}, u32[]{:S(2)}) copy-start(bf16[256,3072]{1,0:T(8,128)(2,1)} %w.5) | copy-start | bytes 4718596
  82.3 27.0 %copy-start.3 = (f32[256,512]{1,0:T(8,128)S(1)}, f32[256,512]{1,0:T(8,128)}, u32[]{:S(2)}) copy-start(f32[256,512]{1,0:T(8,128)} %get-tuple-element.26.kept) | copy-start | bytes 1572868
  82.3 27.0 %collective-permute-start.7 = (bf16[256,512]{1,0:T(8,128)(2,1)S(1)}, bf16[256,512]{1,0:T(8,128)(2,1)S(1)}, u32[]{:S(2)}, u32[]{:S(2)}) collective-permute-start(bf16[256,512]{1,0:T(8,128)(2,1)S(1)} %get-tuple-element.27), channel_id=1, source_target_pairs={{0,1},{1,0},{2,3},{3,2},{4,5},{5,4},{6,7},{7,6},{8,9},{9,8},{10,11... | collective-permute-start | bytes 786440 | tf_op jit(solution)/shard_map/ppermute | solution.py:415
  108.1 5.5 %copy-start.2 = (f32[256,512]{1,0:T(8,128)S(1)}, f32[256,512]{1,0:T(8,128)}, u32[]{:S(2)}) copy-start(f32[256,512]{1,0:T(8,128)} %get-tuple-element.24.kept) | copy-start | bytes 1572868
  108.1 5.5 %collective-permute-start.10 = (bf16[128,512]{1,0:T(8,128)(2,1)S(1)}, bf16[128,512]{1,0:T(8,128)(2,1)S(1)}, u32[]{:S(2)}, u32[]{:S(2)}) collective-permute-start(bf16[128,512]{1,0:T(8,128)(2,1)S(1)} %get-tuple-element.30), channel_id=1, source_target_pairs={{0,1},{1,0},{2,3},{3,2},{4,5},{5,4},{6,7},{7,6},{8,9},{9,8},{10,11... | collective-permute-start | bytes 393224 | tf_op jit(solution)/shard_map/ppermute | solution.py:415
  109.9 37.4 %collective-permute-start.8 = (bf16[128,3072]{1,0:T(8,128)(2,1)S(1)}, bf16[128,3072]{1,0:T(8,128)(2,1)S(1)}, u32[]{:S(2)}, u32[]{:S(2)}) collective-permute-start(bf16[128,3072]{1,0:T(8,128)(2,1)S(1)} %get-tuple-element.28), channel_id=1, source_target_pairs={{0,32},{32,64},{64,96},{96,0},{1,33},{33,65},{65,97},{97,1},{2,34}... | collective-permute-start | bytes 2359304 | tf_op jit(solution)/shard_map/ppermute | solution.py:415
  110.0 37.3 %collective-permute-start.9 = (bf16[128,3072]{1,0:T(8,128)(2,1)S(1)}, bf16[128,3072]{1,0:T(8,128)(2,1)S(1)}, u32[]{:S(2)}, u32[]{:S(2)}) collective-permute-start(bf16[128,3072]{1,0:T(8,128)(2,1)S(1)} %get-tuple-element.29), channel_id=1, source_target_pairs={{0,96},{32,0},{64,32},{96,64},{1,97},{33,1},{65,33},{97,65},{2,98}... | collective-permute-start | bytes 2359304 | tf_op jit(solution)/shard_map/ppermute | solution.py:415
  113.9 33.3 %collective-permute-start.11 = (bf16[128,3072]{1,0:T(8,128)(2,1)S(1)}, bf16[128,3072]{1,0:T(8,128)(2,1)}, u32[]{:S(2)}, u32[]{:S(2)}) collective-permute-start(bf16[128,3072]{1,0:T(8,128)(2,1)S(1)} %shared_out.3), channel_id=1, source_target_pairs={{0,64},{32,96},{64,0},{96,32},{1,65},{33,97},{65,1},{97,33},{2,66}... | collective-permute-start | bytes 2359304 | tf_op jit(solution)/shard_map/ppermute | solution.py:415
  114.7 5.0 %collective-permute-start.6 = (bf16[128,512]{1,0:T(8,128)(2,1)S(1)}, bf16[128,512]{1,0:T(8,128)(2,1)S(1)}, u32[]{:S(2)}, u32[]{:S(2)}) collective-permute-start(bf16[128,512]{1,0:T(8,128)(2,1)S(1)} %get-tuple-element.25), channel_id=1, source_target_pairs={{0,1},{1,0},{2,3},{3,2},{4,5},{5,4},{6,7},{7,6},{8,9},{9,8},{10,11... | collective-permute-start | bytes 393224 | tf_op jit(solution)/shard_map/ppermute | solution.py:415
  119.7 0.7 copy-start.6
  147.2 0.9 copy-start.4
  147.3 1.2 copy-start.5

commit v3 on v2

--- a/solution.py
+++ b/solution.py
@@ -192,15 +192,22 @@
         out[:, j * block : (j + 1) * block] = total.astype(out.dtype)
 
 
-def send_kernel(me, arrived, w, x_out, out, held, sems):
+def swap_halves(first, second):
+    top = iota(first.shape, 1) < CAP
+    lower = jnp.where(top, first, pltpu.roll(second, CAP, 1))
+    upper = jnp.where(top, pltpu.roll(first, CAP, 1), second)
+    return lower, upper
+
+
+def send_kernel(me, arrived, w, x_out, out, held, sems, *, block=512):
     copies = fetch(w, held, sems, 1 - me[0])
-    half = arrived.shape[1]
-    rows = arrived.shape[0] // 2
-    row, col = iota((rows, 2 * rows), 0), iota((rows, 2 * rows), 1)
-    first = ((row >> 2) << 3) + (row & 3)
-    for h in range(2):
-        pick = jnp.where(col == first + h * CAP, 1.0, 0.0).astype(BF)
-        x_out[:, h * half : (h + 1) * half] = dot(pick, arrived[...]).astype(BF)
+    lanes, half = arrived.shape
+    for start in range(0, half, block):
+        tiles = arrived[:, start : start + block].astype(F32)
+        tiles = tiles.reshape(lanes // 16, 2, 8, block)
+        for h, part in enumerate(swap_halves(tiles[:, 0], tiles[:, 1])):
+            cols = slice(h * half + start, h * half + start + block)
+            x_out[:, cols] = part.reshape(lanes // 2, block).astype(BF)
     multiply(x_out, held, copies, out)
 
 
@@ -260,19 +267,18 @@
 def answer_kernel(me, mine, other, w, out, *, block):
     rows, units = mine.shape
     half = out.shape[1]
-    row, col = iota((2 * rows, rows), 0), iota((2 * rows, rows), 1)
-    first = ((col >> 2) << 3) + (col & 3)
-    place = [jnp.where(row == first + h * CAP, 1.0, 0.0).astype(BF) for h in range(2)]
     at_mine = pl.ds(pl.multiple_of(me[0] * units, units), units)
     at_other = pl.ds(pl.multiple_of((1 - me[0]) * units, units), units)
 
     def answer(start):
         cols = slice(start, start + block)
-        return (dot(mine[...], w[at_mine, cols]) + dot(other[...], w[at_other, cols])).astype(BF)
+        total = dot(mine[...], w[at_mine, cols]) + dot(other[...], w[at_other, cols])
+        return total.reshape(rows // 8, 8, block)
 
     for start in range(0, half, block):
-        total = dot(place[0], answer(start)) + dot(place[1], answer(half + start))
-        out[:, start : start + block] = total.astype(BF)
+        parts = swap_halves(answer(start), answer(half + start))
+        both = jnp.stack(parts, axis=1).reshape(2 * rows, block)
+        out[:, start : start + block] = both.astype(BF)
 
 
 def answers(mine, other, w, me, block=768):

time: 152 us -> 151 us (level)
  transfers between devices with their start and end apart: 14 -> 14, of which waited for: 7 -> 7; matrix products, arithmetic and copies ran while one was open for 0% -> 0% of each run, Pallas kernels for 23% -> 22%
where the time goes in v3:
time: 151 us
  waiting for transfers between devices  66.7 us (44%)
  Pallas kernels  44.7 us (30%)
  starting transfers between devices  37.6 us (25%)
  local copies, waits for them, and re-layouts  1.84 us (1%)
    ppermute x12, waiting for transfers between devices, shift(): lax.ppermute(array, axis, [(i, (i + by) % size) for i in range(size)])  56.9 us
    all_to_all x2, starting transfers between devices, exchange(): lax.all_to_all(rows, ('dp', 'expert'), split_axis=0, concat_axis=0, tiled...  21 us
    ppermute x12, starting transfers between devices, shift(): lax.ppermute(array, axis, [(i, (i + by) % size) for i in range(size)])  16.6 us
    pallas_call x1, Pallas kernels, split_gate_up(): pl.pallas_call(functools.partial(split_kernel, sub=sub), grid=(width // d...  12.9 us
    all_to_all x2, waiting for transfers between devices, exchange(): lax.all_to_all(rows, ('dp', 'expert'), split_axis=0, concat_axis=0, tiled...  9.76 us
    pallas_call x2, Pallas kernels, shared_in_part(): pl.pallas_call(functools.partial(shared_kernel, count=len(pieces), cuts=c...  6.88 us
    pallas_call x1, Pallas kernels, keep_half(): pl.pallas_call(keep_kernel, in_specs=[pl.BlockSpec(memory_space=pltpu.SME...  4.17 us
    pallas_call x1, Pallas kernels, send_half(): pl.pallas_call(send_kernel, in_specs=[pl.BlockSpec(memory_space=pltpu.SME...  4.1 us
  transfers between devices with their start and end apart: 14, of which 7 were waited for; matrix products, arithmetic and copies ran while one was open for 0% of the time, Pallas kernels for 22%

profile of v3, /device:TPU:4, one launch (start us, length us, event | category | flops | bytes accessed | tf_op | source)
XLA Modules:
  0.0 150.9 jit_solution(2834566327580775753)
XLA Ops:
  0.0 3.7 %route.1 = bf16[512,1536]{1,0:T(8,128)(2,1)} custom-call(s32[8,128]{1,0:T(8,128)} %bitcast.17, s32[1,64]{1,0:T(1,128)} %bitcast.20, bf16[128,3072]{1,0:T(8,128)(2,1)} %refs_2_.1, bf16[128,3072]{1,0:T(8,128)(2,1)} %refs_2_.1), custom_call_target="tpu_custom_call" | custom-call | tf_op jit(solution)/shard_map/route/pallas_call | solution.py:78
  3.7 11.5 %all-to-all-start = ((bf16[64,8,1536]{2,1,0:T(8,128)(2,1)}), bf16[64,8,1536]{2,1,0:T(8,128)(2,1)S(1)}, u32[]{:S(2)}, u32[]{:S(2)}) async-start(bf16[64,8,1536]{2,1,0:T(8,128)(2,1)} %bitcast.16), calls=%async_computation | async-start | bytes 3145728 | tf_op jit(solution)/shard_map/all_to_all | solution.py:425
  15.2 12.9 %split.1 = (bf16[4,3072,512]{2,1,0:T(8,128)(2,1)}, bf16[2,3072,256]{2,1,0:T(8,128)(2,1)}) custom-call(bf16[3072,2,1024]{2,1,0:T(2,128)(2,1)} %bitcast.15, bf16[3072,2,256]{2,1,0:T(2,128)(2,1)} %w_shared.1), custom_call_target="tpu_custom_call" | custom-call | tf_op jit(solution)/shard_map/split/pallas_call | solution.py:154
  28.1 9.8 %all-to-all-done = bf16[64,8,1536]{2,1,0:T(8,128)(2,1)S(1)} async-done(((bf16[64,8,1536]{2,1,0:T(8,128)(2,1)}), bf16[64,8,1536]{2,1,0:T(8,128)(2,1)S(1)}, u32[]{:S(2)}, u32[]{:S(2)}) %all-to-all-start) | async-done | bytes 1572896 | tf_op jit(solution)/shard_map/all_to_all | solution.py:425
  37.9 4.1 %send_half.1 = (bf16[256,3072]{1,0:T(8,128)(2,1)S(1)}, bf16[256,1024]{1,0:T(8,128)(2,1)S(1)}) custom-call(s32[1]{0:T(128)} %bitcast.3.me, bf16[512,1536]{1,0:T(8,128)(2,1)S(1)} %bitcast.14, bf16[4,3072,512]{2,1,0:T(8,128)(2,1)} %get-tuple-element.18.w), custom_call_target="tpu_custom_call" | custom-call | tf_op jit(solution)/shard_map/send_half/pallas_call | solution.py:222
  42.0 1.3 collective-permute-start
  43.3 0.0 copy-done.1
  43.3 0.0 collective-permute-start.2
  43.3 3.2 %collective-permute-start.3 = (bf16[128,3072]{1,0:T(8,128)(2,1)S(1)}, bf16[128,3072]{1,0:T(8,128)(2,1)}, u32[]{:S(2)}, u32[]{:S(2)}) collective-permute-start(bf16[128,3072]{1,0:T(8,128)(2,1)S(1)} %copy-done.1), channel_id=1, source_target_pairs={{0,96},{32,0},{64,32},{96,64},{1,97},{33,1},{65,33},{97,65},{2,98}... | collective-permute-start | bytes 2359304 | tf_op jit(solution)/shard_map/ppermute | solution.py:421
  46.5 4.2 %keep_half.1.kept = f32[256,1024]{1,0:T(8,128)S(1)} custom-call(s32[1]{0:T(128)} %bitcast.3.me, bf16[256,3072]{1,0:T(8,128)(2,1)S(1)} %get-tuple-element.19.x, bf16[4,3072,512]{2,1,0:T(8,128)(2,1)} %get-tuple-element.18.w), custom_call_target="tpu_custom_call" | custom-call | tf_op jit(solution)/shard_map/keep_half/pallas_call | solution.py:241
  50.7 4.3 %collective-permute-done.came = bf16[256,1024]{1,0:T(8,128)(2,1)S(1)} collective-permute-done((bf16[256,1024]{1,0:T(8,128)(2,1)S(1)}, bf16[256,1024]{1,0:T(8,128)(2,1)S(1)}, u32[]{:S(2)}, u32[]{:S(2)}) %collective-permute-start) | collective-permute-done | bytes 524320 | tf_op jit(solution)/shard_map/ppermute | solution.py:421
  55.0 0.2 activate.1.mine
  55.2 1.3 collective-permute-start.1
  56.4 5.4 %collective-permute-done.1.other = bf16[256,512]{1,0:T(8,128)(2,1)S(1)} collective-permute-done((bf16[256,512]{1,0:T(8,128)(2,1)S(1)}, bf16[256,512]{1,0:T(8,128)(2,1)S(1)}, u32[]{:S(2)}, u32[]{:S(2)}) %collective-permute-start.1) | collective-permute-done | bytes 262176 | tf_op jit(solution)/shard_map/ppermute | solution.py:421
  61.8 0.0 slice-done
  61.8 0.0 slice-done.1
  61.8 3.0 %answers.1 = bf16[512,1536]{1,0:T(8,128)(2,1)} custom-call(s32[1]{0:T(128)} %bitcast.3.me, bf16[256,512]{1,0:T(8,128)(2,1)S(1)} %activate.1.mine, bf16[256,512]{1,0:T(8,128)(2,1)S(1)} %collective-permute-done.1.other, bf16[1024,3072]{1,0:T(8,128)(2,1)S(1)} %bitcast.12), custom_call_target="tpu_custom_call" | custom-call | tf_op jit(solution)/shard_map/answers/pallas_call | solution.py:287
  64.9 9.5 %all-to-all-start.1 = ((bf16[64,8,1536]{2,1,0:T(8,128)(2,1)}), bf16[64,8,1536]{2,1,0:T(8,128)(2,1)S(1)}, u32[]{:S(2)}, u32[]{:S(2)}) async-start(bf16[64,8,1536]{2,1,0:T(8,128)(2,1)} %bitcast.8), calls=%async_computation.1 | async-start | bytes 3145728 | tf_op jit(solution)/shard_map/all_to_all | solution.py:425
  74.4 0.0 collective-permute-done.2.refs_0_
  74.4 0.0 collective-permute-done.3.refs_1_
  74.4 3.5 %shared_in.2 = (f32[256,512]{1,0:T(8,128)}, bf16[256,512]{1,0:T(8,128)(2,1)S(1)}, bf16[64,3072]{1,0:T(8,128)(2,1)S(1)}, bf16[64,3072]{1,0:T(8,128)(2,1)S(1)}) custom-call(bf16[128,3072]{1,0:T(8,128)(2,1)S(1)} %collective-permute-done.2.refs_0_, bf16[128,3072]{1,0:T(8,128)(2,1)} %collective-permute-done.3.refs_1_, ...), custom_call_target="tpu_custom_call" | custom-call | tf_op jit(solution)/shard_map/shared_in/pallas_call | solution.py:328
  78.0 1.5 collective-permute-start.4
  79.4 1.8 %collective-permute-start.5 = (bf16[64,3072]{1,0:T(8,128)(2,1)S(1)}, bf16[64,3072]{1,0:T(8,128)(2,1)S(1)}, u32[]{:S(2)}, u32[]{:S(2)}) collective-permute-start(bf16[64,3072]{1,0:T(8,128)(2,1)S(1)} %get-tuple-element.23), channel_id=1, source_target_pairs={{0,96},{32,0},{64,32},{96,64},{1,97},{33,1},{65,33},{97,65},{2,98}... | collective-permute-start | bytes 1179656 | tf_op jit(solution)/shard_map/ppermute | solution.py:421
  81.2 1.2 collective-permute-start.7
  82.4 21.3 %collective-permute-done.4.refs_0_ = bf16[64,3072]{1,0:T(8,128)(2,1)S(1)} collective-permute-done((bf16[64,3072]{1,0:T(8,128)(2,1)S(1)}, bf16[64,3072]{1,0:T(8,128)(2,1)S(1)}, u32[]{:S(2)}, u32[]{:S(2)}) %collective-permute-start.4) | collective-permute-done | bytes 393248 | tf_op jit(solution)/shard_map/ppermute | solution.py:421
  103.7 0.0 collective-permute-done.5.refs_1_
  103.7 3.3 %shared_in.3 = (f32[256,512]{1,0:T(8,128)}, bf16[128,512]{1,0:T(8,128)(2,1)S(1)}, bf16[128,512]{1,0:T(8,128)(2,1)S(1)}) custom-call(bf16[64,3072]{1,0:T(8,128)(2,1)S(1)} %collective-permute-done.4.refs_0_, bf16[64,3072]{1,0:T(8,128)(2,1)S(1)} %collective-permute-done.5.refs_1_, bf16[128,3072]{1,0:T(8,128)(2,1)S(1)} %copy-done.1, ...), custom_call_target="tpu_custom_call" | custom-call | tf_op jit(solution)/shard_map/shared_in/pallas_call | solution.py:328
  107.0 1.2 collective-permute-start.10
  108.2 0.0 collective-permute-done.7.came
  108.2 0.0 copy-done
  108.2 0.6 shared_out.2
  108.8 0.1 collective-permute-start.8
  108.9 3.2 %collective-permute-start.9 = (bf16[128,3072]{1,0:T(8,128)(2,1)S(1)}, bf16[128,3072]{1,0:T(8,128)(2,1)S(1)}, u32[]{:S(2)}, u32[]{:S(2)}) collective-permute-start(bf16[128,3072]{1,0:T(8,128)(2,1)S(1)} %get-tuple-element.29), channel_id=1, source_target_pairs={{0,96},{32,0},{64,32},{96,64},{1,97},{33,1},{65,33},{97,65},{2,98}... | collective-permute-start | bytes 2359304 | tf_op jit(solution)/shard_map/ppermute | solution.py:421
  112.1 0.3 collective-permute-done.10.came
  112.5 0.4 shared_out.3
  112.9 0.7 collective-permute-start.11
  113.6 1.2 collective-permute-start.6
  114.8 2.5 %combine_gates.1.gates = bf16[2,256,512]{2,1,0:T(8,128)(2,1)} custom-call(s32[8,128]{1,0:T(8,128)} %bitcast.18, s32[8,128]{1,0:T(8,128)} %bitcast.19, s32[1,64]{1,0:T(1,128)} %bitcast.21), custom_call_target="tpu_custom_call" | custom-call | tf_op jit(solution)/shard_map/combine_gates/pallas_call | solution.py:114
  117.3 1.3 collective-permute-done.6.came
  118.6 0.7 copy-done.6
  119.3 2.7 %own_sum.1.base = f32[128,3072]{1,0:T(8,128)} custom-call(f32[256,512]{1,0:T(8,128)} %get-tuple-element.24.kept, bf16[128,512]{1,0:T(8,128)(2,1)} %copy-done.6, bf16[256,3072]{1,0:T(8,128)(2,1)} %w.5), custom_call_target="tpu_custom_call" | custom-call | tf_op jit(solution)/shard_map/own_sum/pallas_call | solution.py:377
  121.9 24.2 %collective-permute-done.8.a = bf16[128,3072]{1,0:T(8,128)(2,1)S(1)} collective-permute-done((bf16[128,3072]{1,0:T(8,128)(2,1)S(1)}, bf16[128,3072]{1,0:T(8,128)(2,1)S(1)}, u32[]{:S(2)}, u32[]{:S(2)}) %collective-permute-start.8) | collective-permute-done | bytes 786464 | tf_op jit(solution)/shard_map/ppermute | solution.py:421
  146.2 0.0 collective-permute-done.9.b
  146.2 0.0 collective-permute-done.11.c
  146.2 0.0 all-to-all-done.1
  146.2 0.9 copy-done.4
  147.1 0.3 copy-done.5
  147.4 3.5 %mix.1 = bf16[128,3072]{1,0:T(8,128)(2,1)} custom-call(bf16[2,256,512]{2,1,0:T(8,128)(2,1)} %combine_gates.1.gates, bf16[512,1536]{1,0:T(8,128)(2,1)S(1)} %bitcast.13, f32[128,3072]{1,0:T(8,128)} %own_sum.1.base, bf16[128,3072]{1,0:T(8,128)(2,1)} %copy-done.4, bf16[128,3072]{1,0:T(8,128)(2,1)} %copy-done.5, bf16[128,3072]{1,0:T(8,128)(2,1)} %collective-permute-done.11.c), custom_call_target="tpu_custom_call" | custom-call | tf_op jit(solution)/shard_map/mix/pallas_call | solution.py:404
  (12 shorter events, 0.0 us)
Async XLA Ops:
  3.7 34.2 %all-to-all-start = ((bf16[64,8,1536]{2,1,0:T(8,128)(2,1)}), bf16[64,8,1536]{2,1,0:T(8,128)(2,1)S(1)}, u32[]{:S(2)}, u32[]{:S(2)}) async-start(bf16[64,8,1536]{2,1,0:T(8,128)(2,1)} %bitcast.16), calls=%async_computation | async-start | bytes 3145728 | tf_op jit(solution)/shard_map/all_to_all | solution.py:425
  37.9 5.4 %copy-start.1 = (bf16[128,3072]{1,0:T(8,128)(2,1)S(1)}, bf16[128,3072]{1,0:T(8,128)(2,1)}, u32[]{:S(2)}) copy-start(bf16[128,3072]{1,0:T(8,128)(2,1)} %refs_2_.1) | copy-start | bytes 2359300
  42.0 13.0 %collective-permute-start = (bf16[256,1024]{1,0:T(8,128)(2,1)S(1)}, bf16[256,1024]{1,0:T(8,128)(2,1)S(1)}, u32[]{:S(2)}, u32[]{:S(2)}) collective-permute-start(bf16[256,1024]{1,0:T(8,128)(2,1)S(1)} %get-tuple-element.20), channel_id=1, source_target_pairs={{0,1},{1,0},{2,3},{3,2},{4,5},{5,4},{6,7},{7,6},{8,9},{9,8},{10,11... | collective-permute-start | bytes 1572872 | tf_op jit(solution)/shard_map/ppermute | solution.py:421
  43.3 31.1 %collective-permute-start.2 = (bf16[128,3072]{1,0:T(8,128)(2,1)S(1)}, bf16[128,3072]{1,0:T(8,128)(2,1)S(1)}, u32[]{:S(2)}, u32[]{:S(2)}) collective-permute-start(bf16[128,3072]{1,0:T(8,128)(2,1)S(1)} %copy-done.1), channel_id=1, source_target_pairs={{0,32},{32,64},{64,96},{96,0},{1,33},{33,65},{65,97},{97,1},{2,34}... | collective-permute-start | bytes 2359304 | tf_op jit(solution)/shard_map/ppermute | solution.py:421
  43.3 31.1 %collective-permute-start.3 = (bf16[128,3072]{1,0:T(8,128)(2,1)S(1)}, bf16[128,3072]{1,0:T(8,128)(2,1)}, u32[]{:S(2)}, u32[]{:S(2)}) collective-permute-start(bf16[128,3072]{1,0:T(8,128)(2,1)S(1)} %copy-done.1), channel_id=1, source_target_pairs={{0,96},{32,0},{64,32},{96,64},{1,97},{33,1},{65,33},{97,65},{2,98}... | collective-permute-start | bytes 2359304 | tf_op jit(solution)/shard_map/ppermute | solution.py:421
  46.5 15.3 %slice-start = ((s8[6291456]{0:T(1024)(128)(4,1)}), s8[4194304]{0:T(1024)(128)(4,1)S(1)}, s32[]{:S(2)}) async-start(s8[6291456]{0:T(1024)(128)(4,1)} %bitcast.10), calls=%async_computation.2 | async-start | bytes 8388608
  46.5 15.3 %slice-start.1 = ((s8[6291456]{0:T(1024)(128)(4,1)}), s8[2097152]{0:T(1024)(128)(4,1)S(1)}, s32[]{:S(2)}) async-start(s8[6291456]{0:T(1024)(128)(4,1)} %bitcast.10), calls=%async_computation.3 | async-start | bytes 4194304
  55.2 6.7 %collective-permute-start.1 = (bf16[256,512]{1,0:T(8,128)(2,1)S(1)}, bf16[256,512]{1,0:T(8,128)(2,1)S(1)}, u32[]{:S(2)}, u32[]{:S(2)}) collective-permute-start(bf16[256,512]{1,0:T(8,128)(2,1)S(1)} %activate.1.mine), channel_id=1, source_target_pairs={{0,1},{1,0},{2,3},{3,2},{4,5},{5,4},{6,7},{7,6},{8,9},{9,8},{10,11... | collective-permute-start | bytes 786440 | tf_op jit(solution)/shard_map/ppermute | solution.py:421
  64.9 81.3 %all-to-all-start.1 = ((bf16[64,8,1536]{2,1,0:T(8,128)(2,1)}), bf16[64,8,1536]{2,1,0:T(8,128)(2,1)S(1)}, u32[]{:S(2)}, u32[]{:S(2)}) async-start(bf16[64,8,1536]{2,1,0:T(8,128)(2,1)} %bitcast.8), calls=%async_computation.1 | async-start | bytes 3145728 | tf_op jit(solution)/shard_map/all_to_all | solution.py:425
  78.0 25.7 %collective-permute-start.4 = (bf16[64,3072]{1,0:T(8,128)(2,1)S(1)}, bf16[64,3072]{1,0:T(8,128)(2,1)S(1)}, u32[]{:S(2)}, u32[]{:S(2)}) collective-permute-start(bf16[64,3072]{1,0:T(8,128)(2,1)S(1)} %get-tuple-element.22), channel_id=1, source_target_pairs={{0,32},{32,64},{64,96},{96,0},{1,33},{33,65},{65,97},{97,1},{2,34}... | collective-permute-start | bytes 1179656 | tf_op jit(solution)/shard_map/ppermute | solution.py:421
  79.4 24.2 %collective-permute-start.5 = (bf16[64,3072]{1,0:T(8,128)(2,1)S(1)}, bf16[64,3072]{1,0:T(8,128)(2,1)S(1)}, u32[]{:S(2)}, u32[]{:S(2)}) collective-permute-start(bf16[64,3072]{1,0:T(8,128)(2,1)S(1)} %get-tuple-element.23), channel_id=1, source_target_pairs={{0,96},{32,0},{64,32},{96,64},{1,97},{33,1},{65,33},{97,65},{2,98}... | collective-permute-start | bytes 1179656 | tf_op jit(solution)/shard_map/ppermute | solution.py:421
  81.2 27.0 %copy-start = (bf16[256,3072]{1,0:T(8,128)(2,1)S(1)}, bf16[256,3072]{1,0:T(8,128)(2,1)}, u32[]{:S(2)}) copy-start(bf16[256,3072]{1,0:T(8,128)(2,1)} %w.5) | copy-start | bytes 4718596
  81.2 27.0 %copy-start.3 = (f32[256,512]{1,0:T(8,128)S(1)}, f32[256,512]{1,0:T(8,128)}, u32[]{:S(2)}) copy-start(f32[256,512]{1,0:T(8,128)} %get-tuple-element.26.kept) | copy-start | bytes 1572868
  81.2 27.0 %collective-permute-start.7 = (bf16[256,512]{1,0:T(8,128)(2,1)S(1)}, bf16[256,512]{1,0:T(8,128)(2,1)S(1)}, u32[]{:S(2)}, u32[]{:S(2)}) collective-permute-start(bf16[256,512]{1,0:T(8,128)(2,1)S(1)} %get-tuple-element.27), channel_id=1, source_target_pairs={{0,1},{1,0},{2,3},{3,2},{4,5},{5,4},{6,7},{7,6},{8,9},{9,8},{10,11... | collective-permute-start | bytes 786440 | tf_op jit(solution)/shard_map/ppermute | solution.py:421
  107.0 5.5 %copy-start.2 = (f32[256,512]{1,0:T(8,128)S(1)}, f32[256,512]{1,0:T(8,128)}, u32[]{:S(2)}) copy-start(f32[256,512]{1,0:T(8,128)} %get-tuple-element.24.kept) | copy-start | bytes 1572868
  107.0 5.5 %collective-permute-start.10 = (bf16[128,512]{1,0:T(8,128)(2,1)S(1)}, bf16[128,512]{1,0:T(8,128)(2,1)S(1)}, u32[]{:S(2)}, u32[]{:S(2)}) collective-permute-start(bf16[128,512]{1,0:T(8,128)(2,1)S(1)} %get-tuple-element.30), channel_id=1, source_target_pairs={{0,1},{1,0},{2,3},{3,2},{4,5},{5,4},{6,7},{7,6},{8,9},{9,8},{10,11... | collective-permute-start | bytes 393224 | tf_op jit(solution)/shard_map/ppermute | solution.py:421
  108.8 37.4 %collective-permute-start.8 = (bf16[128,3072]{1,0:T(8,128)(2,1)S(1)}, bf16[128,3072]{1,0:T(8,128)(2,1)S(1)}, u32[]{:S(2)}, u32[]{:S(2)}) collective-permute-start(bf16[128,3072]{1,0:T(8,128)(2,1)S(1)} %get-tuple-element.28), channel_id=1, source_target_pairs={{0,32},{32,64},{64,96},{96,0},{1,33},{33,65},{65,97},{97,1},{2,34}... | collective-permute-start | bytes 2359304 | tf_op jit(solution)/shard_map/ppermute | solution.py:421
  108.9 37.3 %collective-permute-start.9 = (bf16[128,3072]{1,0:T(8,128)(2,1)S(1)}, bf16[128,3072]{1,0:T(8,128)(2,1)S(1)}, u32[]{:S(2)}, u32[]{:S(2)}) collective-permute-start(bf16[128,3072]{1,0:T(8,128)(2,1)S(1)} %get-tuple-element.29), channel_id=1, source_target_pairs={{0,96},{32,0},{64,32},{96,64},{1,97},{33,1},{65,33},{97,65},{2,98}... | collective-permute-start | bytes 2359304 | tf_op jit(solution)/shard_map/ppermute | solution.py:421
  112.9 33.3 %collective-permute-start.11 = (bf16[128,3072]{1,0:T(8,128)(2,1)S(1)}, bf16[128,3072]{1,0:T(8,128)(2,1)}, u32[]{:S(2)}, u32[]{:S(2)}) collective-permute-start(bf16[128,3072]{1,0:T(8,128)(2,1)S(1)} %shared_out.3), channel_id=1, source_target_pairs={{0,64},{32,96},{64,0},{96,32},{1,65},{33,97},{65,1},{97,33},{2,66}... | collective-permute-start | bytes 2359304 | tf_op jit(solution)/shard_map/ppermute | solution.py:421
  113.6 5.0 %collective-permute-start.6 = (bf16[128,512]{1,0:T(8,128)(2,1)S(1)}, bf16[128,512]{1,0:T(8,128)(2,1)S(1)}, u32[]{:S(2)}, u32[]{:S(2)}) collective-permute-start(bf16[128,512]{1,0:T(8,128)(2,1)S(1)} %get-tuple-element.25), channel_id=1, source_target_pairs={{0,1},{1,0},{2,3},{3,2},{4,5},{5,4},{6,7},{7,6},{8,9},{9,8},{10,11... | collective-permute-start | bytes 393224 | tf_op jit(solution)/shard_map/ppermute | solution.py:421
  118.6 0.7 copy-start.6
  146.2 0.9 copy-start.4
  146.2 1.2 copy-start.5
